TPU v7x, 128 devices: a whole 4x4x4 slice. The times are simulated.
128 devices in a mesh: row: 8 (over x, core), col: 16 (over z, y).
Axes of the slice: x: 4, y: 4, z: 4, core: 2. Of those that a mesh axis runs over, the one named last changes fastest.
Arguments:
- rhs: float32 [32, 1048576], P(None, ('row', 'col')), may hold values from -12.5 to 12.5
- near_blocks: bfloat16 [16384, 4, 4096], P(('row', 'col')), may hold values from -0.1875 to 0.1875
- near_offsets: int32 [16384, 4], P(('row', 'col')), may hold values from -4 to 4, as said below
- v_factor: bfloat16 [16384, 2048], P(('row', 'col')), may hold values from -0.75 to 0.75
- mix_col: bfloat16 [8, 128, 512, 512], P('row', 'col'), may hold values from -0.25 to 0.25
- mix_row: bfloat16 [8, 256, 256, 256], P('row', 'col'), may hold values from -0.375 to 0.375
- u_factor: bfloat16 [16384, 2048], P(('row', 'col')), may hold values from -0.75 to 0.75
Outputs:
- solution: float32 [32, 1048576], P(None, ('row', 'col'))
- residual: float32 [32, 1048576], P(None, ('row', 'col'))
Inputs may be any that keep to these rules, and one draw needn't show every extreme that they name: `near_offsets`: column 0 is 0; the other entries of a row are distinct and nonzero. In every aligned block of 128 rows some row holds -4 and some row holds 4.
All inputs are finite; a program needn't handle non-finite values.
Results may differ from a plain program's by a relative error of at most 0.0054.
Values may be sent and summed in bfloat16 or wider, within the bound.
No kernel may reach another device: no remote copies, remote signals or barrier semaphores. Data moves between devices by JAX's collectives and lax.ppermute only.
A program may use at most 128 MiB of HBM per device.

v0:
```python
import functools

import jax
import jax.numpy as jnp
from jax import lax
from jax.sharding import Mesh
from jax.sharding import PartitionSpec as P

LEAF = 64
RANK = 32
HALO = 4
ROW_COL = ("row_0", "row_1", "col_0", "col_1")
ROW = ("row_0", "row_1")
COL = ("col_0", "col_1")


def extended(x, sides, width):
    edges = {}
    for axis, dim in sides:
        count, length = (lax.axis_size(axis), x.shape[dim])
        up = [(i, (i + 1) % count) for i in range(count - 1)]
        last = lax.slice_in_dim(x, length - width, length, axis=dim)
        first = lax.slice_in_dim(x, 0, width, axis=dim)
        edges[dim] = (
            lax.ppermute(last, axis, up),
            lax.ppermute(first, axis, [(b, a) for a, b in up]),
        )
    done = []
    for _, dim in sides:
        low, high = edges[dim]
        around = [(width, width) if d in done else (0, 0) for d in range(x.ndim)]
        x = jnp.concatenate([jnp.pad(low, around), x, jnp.pad(high, around)], axis=dim)
        done.append(dim)
    return x


def one_axis_at_a_time(x, axes):
    return functools.reduce(lax.psum, axes, x)


def near_part(vector_bf, near_blocks, near_offsets):
    count_rhs = vector_bf.shape[0]
    leaves = near_offsets.shape[0]
    blocks_per = near_offsets.shape[1]
    padded = extended(vector_bf, ((ROW_COL, 1),), HALO * LEAF)
    padded = padded.reshape(count_rhs, leaves + 2 * HALO, LEAF)
    position = jnp.arange(leaves, dtype=jnp.int32)[:, None] + near_offsets + HALO
    picked = padded[:, position, :]
    blocks = near_blocks.reshape(leaves, blocks_per, LEAF, LEAF)
    result = jnp.einsum("slnu,lnvu->slv", picked, blocks, preferred_element_type=jnp.float32)
    return result.reshape(count_rhs, leaves * LEAF)


def far_part(vector_bf, v_factor, mix_col, mix_row, u_factor):
    count_rhs = vector_bf.shape[0]
    n_row = lax.axis_size(ROW)
    n_col = lax.axis_size(COL)
    leaves = v_factor.shape[0]
    slots = leaves // n_col
    subslots = slots // n_row
    width_col = n_col * RANK
    width_row = n_row * RANK
    local = vector_bf.reshape(count_rhs, leaves, LEAF)
    coeffs = jnp.einsum(
        "slu,luk->lsk",
        local,
        v_factor.reshape(leaves, LEAF, RANK),
        preferred_element_type=jnp.float32,
    ).astype(jnp.bfloat16)
    grouped = coeffs.reshape(n_col, slots, count_rhs * RANK)
    received = lax.all_to_all(grouped, COL, split_axis=0, concat_axis=0, tiled=True)
    first = jnp.einsum(
        "cjsk,jckm->jsm",
        received.reshape(n_col, slots, count_rhs, RANK),
        mix_col.reshape(slots, n_col, RANK, width_col),
        preferred_element_type=jnp.float32,
    )
    first = first.astype(jnp.bfloat16)
    regrouped = lax.all_to_all(first, ROW, split_axis=0, concat_axis=0, tiled=True)
    regrouped = regrouped.reshape(n_row, subslots, count_rhs, n_col, RANK)
    second = jnp.einsum(
        "rjspk,jprkn->jpsn",
        regrouped,
        mix_row.reshape(subslots, n_col, n_row, RANK, width_row),
        preferred_element_type=jnp.float32,
    ).astype(jnp.bfloat16)
    second = second.reshape(subslots, n_col, count_rhs, n_row, RANK)
    expanded = jnp.einsum(
        "jpsqk,jpqku->sjpqu",
        second,
        u_factor.reshape(subslots, n_col, n_row, RANK, LEAF),
        preferred_element_type=jnp.float32,
    )
    return expanded.reshape(count_rhs, leaves * LEAF)


def orthogonal(bases, image):
    partial_sums = [jnp.sum(basis * image, axis=1) for basis in bases] + [
        jnp.sum(image * image, axis=1)
    ]
    joined = one_axis_at_a_time(jnp.stack(partial_sums), ROW_COL)
    sums = joined[:-1]
    rest = image
    for index_basis in range(len(bases)):
        rest = rest - sums[index_basis][:, None] * bases[index_basis]
    length = jnp.sqrt(joined[-1] - jnp.sum(sums * sums, axis=0))
    return (sums, rest, length)


def body(rhs, near_blocks, near_offsets, v_factor, mix_col, mix_row, u_factor):

    def operator(vector):
        vector_bf = vector.astype(jnp.bfloat16)
        return (
            vector
            + near_part(vector_bf, near_blocks, near_offsets)
            + far_part(vector_bf, v_factor, mix_col, mix_row, u_factor)
        )

    rhs_length = jnp.sqrt(one_axis_at_a_time(jnp.sum(rhs * rhs, axis=1), ROW_COL))
    basis_first = rhs / rhs_length[:, None]
    image_first = operator(basis_first)
    proj_first, rest_first, h_two_one = orthogonal((basis_first,), image_first)
    h_one_one = proj_first[0]
    basis_second = rest_first / h_two_one[:, None]
    image_second = operator(basis_second)
    proj_second, rest_second, h_three_two = orthogonal((basis_first, basis_second), image_second)
    h_one_two = proj_second[0]
    h_two_two = proj_second[1]
    m_first = h_one_one * h_one_one + h_two_one * h_two_one
    m_cross = h_one_one * h_one_two + h_two_one * h_two_two
    m_second = h_one_two * h_one_two + h_two_two * h_two_two + h_three_two * h_three_two
    determ = m_first * m_second - m_cross * m_cross
    coef_first = rhs_length * (m_second * h_one_one - m_cross * h_one_two) / determ
    coef_second = rhs_length * (m_first * h_one_two - m_cross * h_one_one) / determ
    solution = coef_first[:, None] * basis_first + coef_second[:, None] * basis_second
    residual = rhs - coef_first[:, None] * image_first - coef_second[:, None] * image_second
    return (solution, residual)


def solution(mesh):
    split = Mesh(mesh.devices.reshape(4, 2, 4, 4), ("row_0", "row_1", "col_0", "col_1"))
    return jax.shard_map(
        body,
        mesh=split,
        in_specs=(
            P(None, ROW_COL),
            P(ROW_COL, None, None),
            P(ROW_COL, None),
            P(ROW_COL, None),
            P(ROW, COL, None, None),
            P(ROW, COL, None, None),
            P(ROW_COL, None),
        ),
        out_specs=(P(None, ROW_COL), P(None, ROW_COL)),
        check_vma=False,
    )
```

profile of v0, /device:TPU:1, one launch (start us, length us, event | category | flops | bytes accessed | tf_op | source)
XLA Modules:
  0.0 281.8 jit_solution(2453957108290351879)
XLA Ops:
  0.7 1.6 multiply_reduce_fusion.5
  2.2 9.3 %psum.84 = f32[32]{0:T(128)S(1)} all-reduce(f32[32]{0:T(128)S(1)} %multiply_reduce_fusion.5), channel_id=1, replica_groups=mesh['row_0'=4,'row_1'=2,'col_0'=4,'col_1'=4] {'row_0'}, use_global_device_ids=true, to_apply=%region_1.0 | all-reduce | flops 32 | bytes 256 | tf_op jit(solution)/shard_map/psum | solution.py:38
  11.5 4.8 %psum.85 = f32[32]{0:T(128)S(1)} all-reduce(f32[32]{0:T(128)S(1)} %psum.84), channel_id=1, replica_groups=mesh['row_0'=4,'row_1'=2,'col_0'=4,'col_1'=4] {'row_1'}, use_global_device_ids=true, to_apply=%region_2.0 | all-reduce | flops 32 | bytes 256 | tf_op jit(solution)/shard_map/psum | solution.py:38
  16.3 9.7 %psum.86 = f32[32]{0:T(128)S(1)} all-reduce(f32[32]{0:T(128)S(1)} %psum.85), channel_id=1, replica_groups=mesh['row_0'=4,'row_1'=2,'col_0'=4,'col_1'=4] {'col_0'}, use_global_device_ids=true, to_apply=%region_3.0 | all-reduce | flops 32 | bytes 256 | tf_op jit(solution)/shard_map/psum | solution.py:38
  26.0 8.7 %psum.87 = f32[32]{0:T(128)S(1)} all-reduce(f32[32]{0:T(128)S(1)} %psum.86), channel_id=1, replica_groups=mesh['row_0'=4,'row_1'=2,'col_0'=4,'col_1'=4] {'col_1'}, use_global_device_ids=true, to_apply=%region_4.0 | all-reduce | flops 32 | bytes 256 | tf_op jit(solution)/shard_map/psum | solution.py:38
  36.1 1.9 collective-permute-start
  38.1 7.0 %collective-permute-start.1 = (bf16[32,256]{1,0:T(8,128)(2,1)S(1)}, bf16[32,256]{1,0:T(8,128)(2,1)S(1)}, u32[]{:S(2)}, u32[]{:S(2)}) collective-permute-start(bf16[32,256]{1,0:T(8,128)(2,1)S(1)} %get-tuple-element.16), channel_id=1, source_target_pairs={{1,0},{2,1},{3,2},{4,3},{5,4},{6,5},{7,6},{8,7},{9,8},{10,9},{11,1... | collective-permute-start | bytes 49160 | tf_op jit(solution)/shard_map/ppermute | solution.py:26
  45.0 2.1 reshape.116
  48.1 2.8 copy.28
  51.0 3.4 %convolution_convert_fusion.1 = bf16[128,32,32]{2,1,0:T(8,128)(2,1)} fusion(bf16[128,64,32]{1,2,0:T(8,128)(2,1)S(1)} %copy.28, bf16[32,128,64]{2,1,0:T(8,128)(2,1)} %reshape.116), kind=kOutput, calls=%fused_computation.7 | convolution fusion | flops 16908288 | bytes 1310720 | tf_op jit(solution)/shard_map/slu,luk->lsk/dot_general | solution.py:64
  54.4 2.9 %reshape.118 = bf16[16,8,1024]{2,1,0:T(8,128)(2,1)} reshape(bf16[128,32,32]{2,1,0:T(8,128)(2,1)} %convolution_convert_fusion.1) | data formatting | bytes 524288 | tf_op jit(solution)/shard_map/reshape | solution.py:70
  57.3 4.5 %all-to-all-start = ((bf16[16,8,1024]{2,1,0:T(8,128)(2,1)}), bf16[16,8,1024]{2,1,0:T(8,128)(2,1)}, u32[]{:S(2)}, u32[]{:S(2)}) async-start(bf16[16,8,1024]{2,1,0:T(8,128)(2,1)} %reshape.118), calls=%async_computation | async-start | bytes 524288 | tf_op jit(solution)/shard_map/all_to_all | solution.py:71
  62.0 7.9 %copy.23 = bf16[128,4,4096]{0,2,1:T(8,128)(2,1)} copy(bf16[128,4,4096]{2,1,0:T(4,128)(2,1)} %param.8) | data formatting | bytes 8388608 | tf_op args[1]
  69.9 13.0 %copy.24 = bf16[128,4,64,64]{3,2,1,0:T(8,128)(2,1)} copy(bf16[128,4,64,64]{0,3,2,1:T(8,128)(2,1)} %bitcast.155) | data formatting | bytes 8388608 | tf_op jit(solution)/shard_map/reshape | solution.py:49
  82.9 2.1 reshape.124
  85.0 2.2 pad_maximum_fusion
  87.2 2.6 reshape.113
  89.8 2.5 copy.22
  92.3 4.4 %gather_fusion = bf16[512,32,64]{2,1,0:T(8,128)(2,1)} fusion(bf16[32,136,64]{2,0,1:T(8,128)(2,1)} %copy.22, s32[1024]{0:T(1024)S(1)} %pad_clamp_fusion), kind=kCustom, calls=%fused_computation | custom fusion | bytes 4196352 | tf_op jit(solution)/shard_map/gather | solution.py:48
  97.8 1.7 reshape.119
  99.6 4.3 %fusion = bf16[8,32,512]{2,1,0:T(8,128)(2,1)} fusion(bf16[16,8,32,32]{3,2,0,1:T(8,128)(2,1)} %reshape.119, bf16[8,16,32,512]{3,2,1,0:T(8,128)(2,1)} %bitcast.151), kind=kOutput, calls=%fused_computation.12 | convolution fusion | flops 134348800 | bytes 4718592 | tf_op jit(solution)/shard_map/cjsk,jckm->jsm/dot_general | solution.py:72
  103.9 7.1 %all-to-all-start.1 = ((bf16[8,32,512]{2,1,0:T(8,128)(2,1)}), bf16[8,32,512]{2,1,0:T(8,128)(2,1)S(1)}, u32[]{:S(2)}, u32[]{:S(2)}) async-start(bf16[8,32,512]{2,1,0:T(8,128)(2,1)} %fusion), calls=%async_computation.1 | async-start | bytes 524288 | tf_op jit(solution)/shard_map/all_to_all | solution.py:79
  111.0 6.9 %convolution_bitcast_fusion.1 = f32[32,128,64]{2,0,1:T(8,128)S(1)} fusion(bf16[32,128,4,64]{3,0,2,1:T(8,128)(2,1)} %bitcast.154, bf16[128,4,64,64]{3,2,1,0:T(8,128)(2,1)} %copy.24), kind=kOutput, calls=%fused_computation.3 | convolution fusion | flops 134217728 | bytes 7340032 | tf_op jit(solution)/shard_map/slnu,lnvu->slv/dot_general | solution.py:50
  117.9 2.6 copy.25
  120.5 2.9 %reshape.115 = f32[32,8192]{1,0:T(8,128)} reshape(f32[32,128,64]{2,1,0:T(8,128)} %copy.25) | data formatting | bytes 2097152 | tf_op jit(solution)/shard_map/reshape | solution.py:51
  123.4 1.6 reshape.121
  125.0 1.8 fusion.2
  128.2 1.6 convolution_bitcast_fusion.3
  129.9 2.6 copy.32
  132.5 3.0 %reshape.125 = f32[32,8192]{1,0:T(8,128)} reshape(f32[32,1,16,8,64]{4,3,2,0,1:T(8,128)} %copy.32) | data formatting | bytes 2097152 | tf_op jit(solution)/shard_map/reshape | solution.py:94
  135.4 2.9 %multiply_reduce_fusion.4 = (f32[32]{0:T(128)S(1)}, f32[32]{0:T(128)S(1)}, f32[32,8192]{1,0:T(8,128)}) fusion(f32[32,8192]{1,0:T(8,128)S(1)} %copy-done.1, f32[32]{0:T(128)S(1)} %sqrt.16, f32[32,8192]{1,0:T(8,128)} %reshape.125, f32[32,8192]{1,0:T(8,128)} %reshape.115), kind=kLoop, calls=%fused_computation.30 | loop fusion | flops 1834944 | bytes 4194688 | tf_op jit(solution)/shard_map/reduce_sum | solution.py:98
  138.4 8.6 %psum.88 = f32[2,32]{1,0:T(2,128)S(1)} all-reduce(f32[2,32]{1,0:T(2,128)S(1)} %pad_maximum_fusion.3), channel_id=1, replica_groups=mesh['row_0'=4,'row_1'=2,'col_0'=4,'col_1'=4] {'row_0'}, use_global_device_ids=true, to_apply=%region_7.8 | all-reduce | flops 64 | bytes 512 | tf_op jit(solution)/shard_map/psum | solution.py:38
  146.9 4.5 %psum.89 = f32[2,32]{1,0:T(2,128)S(1)} all-reduce(f32[2,32]{1,0:T(2,128)S(1)} %psum.88), channel_id=1, replica_groups=mesh['row_0'=4,'row_1'=2,'col_0'=4,'col_1'=4] {'row_1'}, use_global_device_ids=true, to_apply=%region_8.9 | all-reduce | flops 64 | bytes 512 | tf_op jit(solution)/shard_map/psum | solution.py:38
  151.5 8.7 %psum.90 = f32[2,32]{1,0:T(2,128)S(1)} all-reduce(f32[2,32]{1,0:T(2,128)S(1)} %psum.89), channel_id=1, replica_groups=mesh['row_0'=4,'row_1'=2,'col_0'=4,'col_1'=4] {'col_0'}, use_global_device_ids=true, to_apply=%region_9.10 | all-reduce | flops 64 | bytes 512 | tf_op jit(solution)/shard_map/psum | solution.py:38
  160.2 8.4 %psum.91 = f32[2,32]{1,0:T(2,128)S(1)} all-reduce(f32[2,32]{1,0:T(2,128)S(1)} %psum.90), channel_id=1, replica_groups=mesh['row_0'=4,'row_1'=2,'col_0'=4,'col_1'=4] {'col_1'}, use_global_device_ids=true, to_apply=%region_10.11 | all-reduce | flops 64 | bytes 512 | tf_op jit(solution)/shard_map/psum | solution.py:38
  168.6 2.5 fusion.22
  171.9 2.8 reshape.128
  174.6 1.9 collective-permute-start.2
  176.6 7.0 %collective-permute-start.3 = (bf16[32,256]{1,0:T(8,128)(2,1)S(1)}, bf16[32,256]{1,0:T(8,128)(2,1)S(1)}, u32[]{:S(2)}, u32[]{:S(2)}) collective-permute-start(bf16[32,256]{1,0:T(8,128)(2,1)S(1)} %get-tuple-element.14), channel_id=1, source_target_pairs={{1,0},{2,1},{3,2},{4,3},{5,4},{6,5},{7,6},{8,7},{9,8},{10,9},{11,1... | collective-permute-start | bytes 49160 | tf_op jit(solution)/shard_map/ppermute | solution.py:26
  183.5 3.4 %convolution_convert_fusion = bf16[128,32,32]{2,1,0:T(8,128)(2,1)} fusion(bf16[128,64,32]{1,2,0:T(8,128)(2,1)} %copy-done.2, bf16[32,128,64]{2,1,0:T(8,128)(2,1)} %reshape.128), kind=kOutput, calls=%fused_computation.6 | convolution fusion | flops 16908288 | bytes 1310720 | tf_op jit(solution)/shard_map/slu,luk->lsk/dot_general | solution.py:64
  187.0 2.9 %reshape.129 = bf16[16,8,1024]{2,1,0:T(8,128)(2,1)} reshape(bf16[128,32,32]{2,1,0:T(8,128)(2,1)} %convolution_convert_fusion) | data formatting | bytes 524288 | tf_op jit(solution)/shard_map/reshape | solution.py:70
  189.9 4.5 %all-to-all-start.2 = ((bf16[16,8,1024]{2,1,0:T(8,128)(2,1)}), bf16[16,8,1024]{2,1,0:T(8,128)(2,1)}, u32[]{:S(2)}, u32[]{:S(2)}) async-start(bf16[16,8,1024]{2,1,0:T(8,128)(2,1)} %reshape.129), calls=%async_computation.2 | async-start | bytes 524288 | tf_op jit(solution)/shard_map/all_to_all | solution.py:71
  194.4 1.9 pad_maximum_fusion.1
  196.3 2.6 reshape.126
  198.9 2.5 copy.33
  201.4 4.4 %gather_fusion.1 = bf16[512,32,64]{2,1,0:T(8,128)(2,1)} fusion(bf16[32,136,64]{2,0,1:T(8,128)(2,1)} %copy.33, s32[1024]{0:T(1024)S(1)} %pad_clamp_fusion), kind=kCustom, calls=%fused_computation.1 | custom fusion | bytes 4196352 | tf_op jit(solution)/shard_map/gather | solution.py:48
  206.9 1.8 reshape.130
  208.7 4.3 %fusion.1 = bf16[8,32,512]{2,1,0:T(8,128)(2,1)} fusion(bf16[16,8,32,32]{3,2,0,1:T(8,128)(2,1)} %reshape.130, bf16[8,16,32,512]{3,2,1,0:T(8,128)(2,1)} %bitcast.152), kind=kOutput, calls=%fused_computation.13 | convolution fusion | flops 134348800 | bytes 4718592 | tf_op jit(solution)/shard_map/cjsk,jckm->jsm/dot_general | solution.py:72
  213.0 7.3 %all-to-all-start.3 = ((bf16[8,32,512]{2,1,0:T(8,128)(2,1)}), bf16[8,32,512]{2,1,0:T(8,128)(2,1)S(1)}, u32[]{:S(2)}, u32[]{:S(2)}) async-start(bf16[8,32,512]{2,1,0:T(8,128)(2,1)} %fusion.1), calls=%async_computation.3 | async-start | bytes 524288 | tf_op jit(solution)/shard_map/all_to_all | solution.py:79
  220.3 6.9 %convolution_bitcast_fusion = f32[32,128,64]{2,0,1:T(8,128)S(1)} fusion(bf16[32,128,4,64]{3,0,2,1:T(8,128)(2,1)} %bitcast.153, bf16[128,4,64,64]{3,2,1,0:T(8,128)(2,1)} %copy.24), kind=kOutput, calls=%fused_computation.2 | convolution fusion | flops 134217728 | bytes 7340032 | tf_op jit(solution)/shard_map/slnu,lnvu->slv/dot_general | solution.py:50
  227.2 2.6 copy.35
  229.8 2.9 %reshape.127 = f32[32,8192]{1,0:T(8,128)} reshape(f32[32,128,64]{2,1,0:T(8,128)} %copy.35) | data formatting | bytes 2097152 | tf_op jit(solution)/shard_map/reshape | solution.py:51
  232.7 1.6 reshape.131
  234.3 1.8 fusion.3
  236.1 1.4 reshape.132
  237.6 2.0 convolution_bitcast_fusion.2
  239.5 2.6 copy.41
  242.1 2.9 %reshape.133 = f32[32,8192]{1,0:T(8,128)} reshape(f32[32,1,16,8,64]{4,3,2,0,1:T(8,128)} %copy.41) | data formatting | bytes 2097152 | tf_op jit(solution)/shard_map/reshape | solution.py:94
  245.0 3.3 %multiply_reduce_fusion.2 = (f32[32]{0:T(128)S(1)}, f32[32]{0:T(128)S(1)}, f32[32]{0:T(128)S(1)}, f32[32,8192]{1,0:T(8,128)}) fusion(f32[32,8192]{1,0:T(8,128)S(1)} %copy-done.1, f32[32]{0:T(128)S(1)} %sqrt.16, f32[32,8192]{1,0:T(8,128)} %get-tuple-element.9, f32[32,8192]{1,0:T(8,128)} %reshape.133, f32[32,8192]{1,0:T(8,128)} %reshape.127), kind=kLoop, calls=%fused_computation.26 | loop fusion | flops 2359200 | bytes 5243392 | tf_op jit(solution)/shard_map/reduce_sum | solution.py:98
  248.3 8.6 %psum.92 = f32[3,32]{1,0:T(4,128)S(1)} all-reduce(f32[3,32]{1,0:T(4,128)S(1)} %pad_maximum_fusion.2), channel_id=1, replica_groups=mesh['row_0'=4,'row_1'=2,'col_0'=4,'col_1'=4] {'row_0'}, use_global_device_ids=true, to_apply=%region_14.15 | all-reduce | flops 96 | bytes 768 | tf_op jit(solution)/shard_map/psum | solution.py:38
  256.9 4.5 %psum.93 = f32[3,32]{1,0:T(4,128)S(1)} all-reduce(f32[3,32]{1,0:T(4,128)S(1)} %psum.92), channel_id=1, replica_groups=mesh['row_0'=4,'row_1'=2,'col_0'=4,'col_1'=4] {'row_1'}, use_global_device_ids=true, to_apply=%region_15.16 | all-reduce | flops 96 | bytes 768 | tf_op jit(solution)/shard_map/psum | solution.py:38
  261.4 8.5 %psum.94 = f32[3,32]{1,0:T(4,128)S(1)} all-reduce(f32[3,32]{1,0:T(4,128)S(1)} %psum.93), channel_id=1, replica_groups=mesh['row_0'=4,'row_1'=2,'col_0'=4,'col_1'=4] {'col_0'}, use_global_device_ids=true, to_apply=%region_16.17 | all-reduce | flops 96 | bytes 768 | tf_op jit(solution)/shard_map/psum | solution.py:38
  269.9 8.4 %psum.95 = f32[3,32]{1,0:T(4,128)S(1)} all-reduce(f32[3,32]{1,0:T(4,128)S(1)} %psum.94), channel_id=1, replica_groups=mesh['row_0'=4,'row_1'=2,'col_0'=4,'col_1'=4] {'col_1'}, use_global_device_ids=true, to_apply=%region_17.18 | all-reduce | flops 96 | bytes 768 | tf_op jit(solution)/shard_map/psum | solution.py:38
  278.3 3.5 %multiply_subtract_fusion = (f32[32,8192]{1,0:T(8,128)}, f32[32,8192]{1,0:T(8,128)}) fusion(f32[32,8192]{1,0:T(8,128)} %get-tuple-element.7, f32[32,8192]{1,0:T(8,128)S(1)} %copy-done.1, f32[32,8192]{1,0:T(8,128)} %get-tuple-element.10, f32[32]{0:T(128)S(1)} %get-tuple-element.18, f32[32]{0:T(128)S(1)} %get-tuple-element.17, ...), kind=kLoop, calls=%fused_computation.22 | loop fusion | flops 2097152 | bytes 6291840 | tf_op jit(solution)/shard_map/sub | solution.py:137
  (41 shorter events, 7.2 us)
Async XLA Ops:
  0.6 124.4 %copy-start = (bf16[1,16,256,256]{3,2,1,0:T(8,128)(2,1)S(1)}, bf16[1,16,256,256]{3,2,1,0:T(8,128)(2,1)}, u32[]{:S(2)}) copy-start(bf16[1,16,256,256]{3,2,1,0:T(8,128)(2,1)} %param.12) | copy-start | bytes 6291460
  0.6 46.5 %copy-start.6 = (bf16[128,2048]{1,0:T(8,128)(2,1)S(1)}, bf16[128,2048]{1,0:T(8,128)(2,1)}, u32[]{:S(2)}) copy-start(bf16[128,2048]{1,0:T(8,128)(2,1)} %param.10) | copy-start | bytes 1572868
  36.1 12.0 %copy-start.4 = (bf16[32,8192]{1,0:T(8,128)(2,1)}, bf16[32,8192]{1,0:T(8,128)(2,1)S(1)}, u32[]{:S(2)}) copy-start(bf16[32,8192]{1,0:T(8,128)(2,1)S(1)} %fusion.21) | copy-start | bytes 1572868
  36.1 48.8 %collective-permute-start = (bf16[32,256]{1,0:T(8,128)(2,1)S(1)}, bf16[32,256]{1,0:T(8,128)(2,1)S(1)}, u32[]{:S(2)}, u32[]{:S(2)}) collective-permute-start(bf16[32,256]{1,0:T(8,128)(2,1)S(1)} %get-tuple-element.15), channel_id=1, source_target_pairs={{0,1},{1,2},{2,3},{3,4},{4,5},{5,6},{6,7},{7,8},{8,9},{9,10},{10,1... | collective-permute-start | bytes 49160 | tf_op jit(solution)/shard_map/ppermute | solution.py:25
  38.1 46.9 %collective-permute-start.1 = (bf16[32,256]{1,0:T(8,128)(2,1)S(1)}, bf16[32,256]{1,0:T(8,128)(2,1)S(1)}, u32[]{:S(2)}, u32[]{:S(2)}) collective-permute-start(bf16[32,256]{1,0:T(8,128)(2,1)S(1)} %get-tuple-element.16), channel_id=1, source_target_pairs={{1,0},{2,1},{3,2},{4,3},{5,4},{6,5},{7,6},{8,7},{9,8},{10,9},{11,1... | collective-permute-start | bytes 49160 | tf_op jit(solution)/shard_map/ppermute | solution.py:26
  50.9 6.3 %copy-start.2 = (bf16[128,64,32]{1,2,0:T(8,128)(2,1)}, bf16[128,64,32]{1,2,0:T(8,128)(2,1)S(1)}, u32[]{:S(2)}) copy-start(bf16[128,64,32]{1,2,0:T(8,128)(2,1)S(1)} %copy.28) | copy-start | bytes 1572868
  51.0 10.8 %copy-start.7 = (s32[128,4]{0,1:T(4,128)S(1)}, s32[128,4]{0,1:T(4,128)}, u32[]{:S(2)}) copy-start(s32[128,4]{0,1:T(4,128)} %param.9) | copy-start | bytes 6148
  57.3 39.5 %all-to-all-start = ((bf16[16,8,1024]{2,1,0:T(8,128)(2,1)}), bf16[16,8,1024]{2,1,0:T(8,128)(2,1)}, u32[]{:S(2)}, u32[]{:S(2)}) async-start(bf16[16,8,1024]{2,1,0:T(8,128)(2,1)} %reshape.118), calls=%async_computation | async-start | bytes 524288 | tf_op jit(solution)/shard_map/all_to_all | solution.py:71
  84.9 43.3 %copy-start.3 = (bf16[16,8,32,64]{3,2,1,0:T(8,128)(2,1)}, bf16[16,8,32,64]{3,2,1,0:T(8,128)(2,1)S(1)}, u32[]{:S(2)}) copy-start(bf16[16,8,32,64]{3,2,1,0:T(8,128)(2,1)S(1)} %reshape.124) | copy-start | bytes 1572868
  103.9 19.6 %all-to-all-start.1 = ((bf16[8,32,512]{2,1,0:T(8,128)(2,1)}), bf16[8,32,512]{2,1,0:T(8,128)(2,1)S(1)}, u32[]{:S(2)}, u32[]{:S(2)}) async-start(bf16[8,32,512]{2,1,0:T(8,128)(2,1)} %fusion), calls=%async_computation.1 | async-start | bytes 524288 | tf_op jit(solution)/shard_map/all_to_all | solution.py:79
  132.5 3.0 %copy-start.1 = (f32[32,8192]{1,0:T(8,128)S(1)}, f32[32,8192]{1,0:T(8,128)}, u32[]{:S(2)}) copy-start(f32[32,8192]{1,0:T(8,128)} %param.7) | copy-start | bytes 3145732
  171.1 0.8 copy-start.5
  174.6 19.7 %collective-permute-start.2 = (bf16[32,256]{1,0:T(8,128)(2,1)S(1)}, bf16[32,256]{1,0:T(8,128)(2,1)S(1)}, u32[]{:S(2)}, u32[]{:S(2)}) collective-permute-start(bf16[32,256]{1,0:T(8,128)(2,1)S(1)} %get-tuple-element.13), channel_id=1, source_target_pairs={{0,1},{1,2},{2,3},{3,4},{4,5},{5,6},{6,7},{7,8},{8,9},{9,10},{10,1... | collective-permute-start | bytes 49160 | tf_op jit(solution)/shard_map/ppermute | solution.py:25
  176.6 17.8 %collective-permute-start.3 = (bf16[32,256]{1,0:T(8,128)(2,1)S(1)}, bf16[32,256]{1,0:T(8,128)(2,1)S(1)}, u32[]{:S(2)}, u32[]{:S(2)}) collective-permute-start(bf16[32,256]{1,0:T(8,128)(2,1)S(1)} %get-tuple-element.14), channel_id=1, source_target_pairs={{1,0},{2,1},{3,2},{4,3},{5,4},{6,5},{7,6},{8,7},{9,8},{10,9},{11,1... | collective-permute-start | bytes 49160 | tf_op jit(solution)/shard_map/ppermute | solution.py:26
  189.9 15.9 %all-to-all-start.2 = ((bf16[16,8,1024]{2,1,0:T(8,128)(2,1)}), bf16[16,8,1024]{2,1,0:T(8,128)(2,1)}, u32[]{:S(2)}, u32[]{:S(2)}) async-start(bf16[16,8,1024]{2,1,0:T(8,128)(2,1)} %reshape.129), calls=%async_computation.2 | async-start | bytes 524288 | tf_op jit(solution)/shard_map/all_to_all | solution.py:71
  213.0 19.7 %all-to-all-start.3 = ((bf16[8,32,512]{2,1,0:T(8,128)(2,1)}), bf16[8,32,512]{2,1,0:T(8,128)(2,1)S(1)}, u32[]{:S(2)}, u32[]{:S(2)}) async-start(bf16[8,32,512]{2,1,0:T(8,128)(2,1)} %fusion.1), calls=%async_computation.3 | async-start | bytes 524288 | tf_op jit(solution)/shard_map/all_to_all | solution.py:79
where the time goes:
time: 287 us; the launch traced here: 282 us
  blocking collectives  92.7 us (32%)
  local copies, waits for them, and re-layouts  91.4 us (32%)
  starting transfers between devices  41.1 us (14%)
  matrix products  36.4 us (13%)
  other arithmetic  19.3 us (7%)
    psum x12, blocking collectives, one_axis_at_a_time(): return functools.reduce(lax.psum, axes, x)  92.7 us
    all_to_all x2, starting transfers between devices, far_part(): lax.all_to_all(first, ROW, split_axis=0, concat_axis=0, tiled=True)  14.4 us
    ppermute x2, starting transfers between devices, extended(): lax.ppermute(first, axis, [(b, a) for a, b in up])  13.9 us
    dot_general x2, matrix products, near_part(): jnp.einsum('slnu,lnvu->slv', picked, blocks, preferred_element_type=jnp.f...  13.9 us
    reshape x1, local copies, waits for them, and re-layouts, near_part(): blocks = near_blocks.reshape(leaves, blocks_per, LEAF, LEAF)  13 us
    reshape x4, local copies, waits for them, and re-layouts, near_part(): padded = padded.reshape(count_rhs, leaves + 2 * HALO, LEAF)  10.2 us
    unnamed x18, local copies, waits for them, and re-layouts  9.72 us
    all_to_all x2, starting transfers between devices, far_part(): lax.all_to_all(grouped, COL, split_axis=0, concat_axis=0, tiled=True)  8.99 us
  transfers between devices with their start and end apart: 8, of which 0 were waited for; matrix products, arithmetic and copies ran while one was open for 32% of the time, Pallas kernels for 0%

commit v1 on v0

v1 whole, which is shorter than its diff:
```python
import functools

import jax
import jax.numpy as jnp
from jax import lax
from jax.experimental import pallas as pl
from jax.experimental.pallas import tpu as pltpu
from jax.sharding import Mesh
from jax.sharding import PartitionSpec as P

LEAF = 64
RANK = 32
HALO = 4
RHS = 32
LANES = 128
ROW_COL = ("row_0", "row_1", "col_0", "col_1")
ROW = ("row_0", "row_1")
COL = ("col_0", "col_1")
F32 = jnp.float32
BF16 = jnp.bfloat16


def dot(a, b):
    return jnp.dot(a, b, preferred_element_type=F32)


def dot_t(a, b):
    return lax.dot_general(a, b, (((1,), (1,)), ((), ())), preferred_element_type=F32)


def lane_group(rows):
    return lax.broadcasted_iota(jnp.int32, (rows, LANES), 1) // RANK


def lane_half(rows):
    return lax.broadcasted_iota(jnp.int32, (rows, LANES), 1) < LEAF


def spread_v_kernel(rhs_ref, v_ref, turn_ref, vbd_ref, z_ref, low_ref, high_ref, scratch):
    group = lane_group(16)
    shift = turn_ref[0] * RANK
    groups = vbd_ref.shape[0]
    for g in range(groups):
        slot = g % scratch.shape[0]
        for leaf in range(4):
            x = v_ref[4 * g + leaf].astype(F32)
            for ur in range(4):
                turned = x if leaf == ur else pltpu.roll(x, (leaf - ur) * RANK % LANES, 1)
                scratch[slot, pl.ds(leaf * LEAF + ur, 16, stride=4), :] = jnp.where(group == leaf, turned, 0.0)
        vbd_ref[g] = scratch[slot].astype(BF16)
    for g in range(groups):
        part = dot(rhs_ref[:, 256 * g : 256 * (g + 1)].astype(BF16), vbd_ref[g])
        z_ref[g // 2, :, (g % 2) * LANES : (g % 2 + 1) * LANES] = pltpu.roll(part, shift, 1).astype(BF16)
    edge = HALO * LEAF
    low_ref[...] = rhs_ref[:, :edge].astype(BF16)
    high_ref[...] = rhs_ref[:, rhs_ref.shape[1] - edge :].astype(BF16)


def spread_near_kernel(near_ref, out_ref, rows, wide):
    half = lane_half(32)
    for leaf in range(near_ref.shape[0]):
        rows[leaf] = near_ref[leaf].astype(F32)
        for h in range(2):
            even = rows[leaf, pl.ds(2 * h, 32, stride=4), :]
            odd = rows[leaf, pl.ds(2 * h + 1, 32, stride=4), :]
            wide[leaf, h, pl.ds(0, 32, stride=2), :] = jnp.where(half, even, pltpu.roll(odd, LEAF, 1))
            wide[leaf, h, pl.ds(1, 32, stride=2), :] = jnp.where(half, pltpu.roll(even, LEAF, 1), odd)
            out_ref[leaf // 2, (leaf % 2) * LEAF : (leaf % 2 + 1) * LEAF, h * LANES : (h + 1) * LANES] = wide[leaf, h].astype(BF16)


def spread_u_kernel(u_ref, out_ref, scratch):
    half = lane_half(16)
    zero = jnp.zeros((RANK, LANES), F32)
    for g in range(out_ref.shape[0]):
        slot = g % scratch.shape[0]
        for leaf in range(4):
            x = u_ref[4 * g + leaf].astype(F32)
            other = pltpu.roll(x, LEAF, 1)
            tile = leaf // 2
            keep = half if leaf % 2 == 0 else ~half
            for kp in range(2):
                scratch[slot, tile, pl.ds(leaf * RANK + kp, 16, stride=2), :] = jnp.where(
                    keep, x if kp == leaf % 2 else other, 0.0
                )
            scratch[slot, 1 - tile, leaf * RANK : (leaf + 1) * RANK, :] = zero
        for tile in range(2):
            out_ref[g, :, tile * LANES : (tile + 1) * LANES] = scratch[slot, tile].astype(BF16)


def near_kernel(v_ref, low_ref, high_ref, place_ref, near_ref, out_ref, plain, swapped):
    half = lane_half(RHS)
    edge = HALO // 2
    tiles = v_ref.shape[1] // LANES

    def put(t, x):
        plain[t] = x.astype(BF16)
        swapped[t] = pltpu.roll(x, LEAF, 1).astype(BF16)

    for t in range(edge):
        put(t, low_ref[:, t * LANES : (t + 1) * LANES].astype(F32))
        put(edge + tiles + t, high_ref[:, t * LANES : (t + 1) * LANES].astype(F32))
    for t in range(tiles):
        put(edge + t, v_ref[:, t * LANES : (t + 1) * LANES])

    def pick(block, leaf, side):
        place = place_ref[block, leaf]
        tile = place // 2
        odd = place % 2
        x = jnp.where(odd == side, plain[tile].astype(F32), swapped[tile].astype(F32))
        return x

    def one(pair):
        rows = []
        for par in range(2):
            leaf = 2 * pair + par
            tiles_of = [
                jnp.where(half, pick(2 * h, leaf, 0), pick(2 * h + 1, leaf, 1)).astype(BF16)
                for h in range(2)
            ]
            rows.append(jnp.concatenate(tiles_of, axis=1))
        both = dot_t(jnp.concatenate(rows, axis=0), near_ref[pair])
        return jnp.where(half, both[:RHS], both[RHS:])

    for pair in range(near_ref.shape[0]):
        out_ref[:, pair * LANES : (pair + 1) * LANES] = one(pair)


def gather_lanes(parts, where_from, group):
    x = parts[(0 - where_from) % 4]
    for q in range(1, 4):
        x = jnp.where(group == q, parts[(q - where_from) % 4], x)
    return x


def turned_rows(ref_rows, count, where_from):
    order = [4 * four + (q - where_from) % 4 for four in range(count // 4) for q in range(4)]
    return jnp.concatenate([ref_rows[c * RANK : (c + 1) * RANK] for c in order], axis=0)


def first_mix_kernel(z_ref, mix_ref, turn_ref, out_ref):
    n_col = z_ref.shape[0]
    group = lane_group(RHS)
    shift = turn_ref[0] * RANK
    for j in range(mix_ref.shape[0]):
        tile = j // 4
        lhs = jnp.concatenate(
            [
                gather_lanes(
                    [z_ref[4 * four + c, :, tile * LANES : (tile + 1) * LANES] for c in range(4)], j % 4, group
                )
                for four in range(n_col // 4)
            ],
            axis=1,
        )
        out = dot(lhs, turned_rows(mix_ref[j], n_col, j % 4))
        for t in range(out.shape[1] // LANES):
            out_ref[j, :, t * LANES : (t + 1) * LANES] = pltpu.roll(
                out[:, t * LANES : (t + 1) * LANES], shift, 1
            ).astype(BF16)


def second_mix(t1_ref, mix_ref, t2_ref):
    n_row = t1_ref.shape[0]
    group = lane_group(RHS)
    for p in range(mix_ref.shape[0]):
        tile = p // 4
        lhs = jnp.concatenate(
            [
                gather_lanes(
                    [t1_ref[4 * four + r, :, tile * LANES : (tile + 1) * LANES] for r in range(4)], p % 4, group
                )
                for four in range(n_row // 4)
            ],
            axis=1,
        )
        t2_ref[p] = dot(lhs, turned_rows(mix_ref[p], n_row, p % 4)).astype(BF16)


def far_tile(t2_ref, ubd_ref, g):
    return dot(t2_ref[g // 2, :, (g % 2) * LANES : (g % 2 + 1) * LANES], ubd_ref[g])


def second_mix_kernel(t1_ref, mix_ref, ubd_ref, near_ref, vbd_ref, turn_ref, d_ref, z_ref, low_ref, high_ref, t2_ref):
    second_mix(t1_ref, mix_ref, t2_ref)
    shift = turn_ref[0] * RANK
    groups = ubd_ref.shape[0]
    for g in range(groups):
        lanes = slice(256 * g, 256 * (g + 1))
        d_ref[:, lanes] = far_tile(t2_ref, ubd_ref, g) + near_ref[:, lanes]
    for g in range(groups):
        lanes = slice(256 * g, 256 * (g + 1))
        part = dot(d_ref[:, lanes].astype(BF16), vbd_ref[g])
        z_ref[g // 2, :, (g % 2) * LANES : (g % 2 + 1) * LANES] = pltpu.roll(part, shift, 1).astype(BF16)
    edge = HALO * LEAF
    low_ref[...] = d_ref[:, :edge].astype(BF16)
    high_ref[...] = d_ref[:, d_ref.shape[1] - edge :].astype(BF16)


def last_mix_kernel(t1_ref, mix_ref, ubd_ref, near_ref, rhs_ref, d_ref, e_ref, sums_ref, t2_ref):
    second_mix(t1_ref, mix_ref, t2_ref)
    total = [jnp.zeros((RHS, LANES), F32) for _ in range(6)]
    for g in range(ubd_ref.shape[0]):
        wide = far_tile(t2_ref, ubd_ref, g) + near_ref[:, 256 * g : 256 * (g + 1)]
        e_ref[:, 256 * g : 256 * (g + 1)] = wide
        for t in range(2):
            lanes = slice(256 * g + LANES * t, 256 * g + LANES * (t + 1))
            r, d, e = rhs_ref[:, lanes], d_ref[:, lanes], wide[:, LANES * t : LANES * (t + 1)]
            terms = (r * r, r * d, d * d, r * e, d * e, e * e)
            total = [a + b for a, b in zip(total, terms)]
    stacked = jnp.concatenate(total + [jnp.zeros((2 * RHS, LANES), F32)], axis=0)
    row = jnp.sum(stacked.T, axis=0, keepdims=True)
    sums_ref[...] = jnp.broadcast_to(row, sums_ref.shape)


def finish_kernel(sums_ref, rhs_ref, d_ref, e_ref, solution_ref, residual_ref):
    row = jnp.sum(sums_ref[...], axis=0, keepdims=True)
    columns = jnp.broadcast_to(row, (LANES, row.shape[1])).T
    rr, rd, dd, re, de, ee = [columns[i * RHS : (i + 1) * RHS] for i in range(6)]
    scale = 1.0 / rr
    alpha = rd * scale
    h21_sq = (dd - alpha * rd) * scale
    h11 = 1.0 + alpha
    cross = re * scale - alpha * alpha
    inverse = 1.0 / h21_sq
    gain = ((de - alpha * dd - alpha * re + alpha * (alpha * rd)) * scale) * inverse
    h22 = 1.0 + gain
    spread = ((ee - 2.0 * alpha * de + alpha * (alpha * dd)) * scale) * inverse
    h32_sq = spread - gain * gain - cross * (cross * inverse)
    minor = h11 * h22 - cross
    determ = minor * minor + h32_sq * (h11 * h11 + h21_sq)
    x_first = (h22 * minor + h11 * h32_sq) / determ
    x_second = -minor / determ
    on_rhs = x_first - alpha * x_second
    on_d = x_first + x_second * (1.0 - alpha)
    for t in range(rhs_ref.shape[1] // LANES):
        lanes = slice(t * LANES, (t + 1) * LANES)
        r, d, e = rhs_ref[:, lanes], d_ref[:, lanes], e_ref[:, lanes]
        solution_ref[:, lanes] = on_rhs * r + x_second * d
        residual_ref[:, lanes] = (1.0 - on_rhs) * r - on_d * d - x_second * e


VMEM = pl.BlockSpec(memory_space=pltpu.VMEM)
SMEM = pl.BlockSpec(memory_space=pltpu.SMEM)


def shape(dims, dtype):
    return jax.ShapeDtypeStruct(dims, dtype)


def call(kernel, in_specs, outs, scratch=(), flops=1_000_000, **more):
    out_specs = jax.tree.map(lambda _: VMEM, outs)
    return pl.pallas_call(
        kernel,
        in_specs=in_specs,
        out_shape=outs,
        out_specs=more.pop("out_specs", out_specs),
        scratch_shapes=list(scratch),
        cost_estimate=pl.CostEstimate(flops=flops, bytes_accessed=1_000_000, transcendentals=0),
        name=kernel.__name__,
        **more,
    )


def body(rhs, near_blocks, near_offsets, v_factor, mix_col, mix_row, u_factor):
    count = rhs.shape[1]
    leaves = near_offsets.shape[0]
    n_row = lax.axis_size(ROW)
    n_col = lax.axis_size(COL)
    devices = n_row * n_col
    slots = leaves // n_col
    groups = leaves // 4
    width_col = n_col * RANK
    turn_col = (lax.axis_index(COL) % 4).astype(jnp.int32).reshape(1)
    turn_row = (lax.axis_index(ROW) % 4).astype(jnp.int32).reshape(1)
    place = near_offsets.T + (jnp.arange(leaves, dtype=jnp.int32) + HALO)[None, :]
    near_rows = (
        near_blocks.reshape(leaves, 4, 32, LANES).transpose(0, 2, 1, 3).reshape(leaves, LANES, LANES)
    )
    z_shape = shape((n_col, RHS, slots * RANK), BF16)
    edge_shape = shape((RHS, HALO * LEAF), BF16)
    field = shape((RHS, count), F32)

    def halos(low, high):
        up = [(i, i + 1) for i in range(devices - 1)]
        down = [(b, a) for a, b in up]
        return lax.ppermute(high, ROW_COL, up), lax.ppermute(low, ROW_COL, down)

    def exchange(x, axes):
        return lax.all_to_all(x, axes, split_axis=0, concat_axis=0, tiled=True)

    def near(v, below, above):
        return call(
            near_kernel,
            [VMEM, VMEM, VMEM, SMEM, VMEM],
            field,
            [pltpu.VMEM((leaves // 2 + HALO, RHS, LANES), BF16)] * 2,
        )(v, below, above, place, near_wide)

    def first_mix(z):
        return call(
            first_mix_kernel, [VMEM, VMEM, SMEM], shape((n_row, RHS, width_col), BF16)
        )(z, mix_col.reshape(slots, width_col, width_col), turn_row)

    mix_second = mix_row.reshape(n_col, n_row * RANK, n_row * RANK)
    t2_scratch = [pltpu.VMEM((n_col, RHS, n_row * RANK), BF16)]

    v_wide, z, low, high = call(
        spread_v_kernel,
        [VMEM, VMEM, SMEM],
        (shape((groups, 4 * LEAF, 4 * RANK), BF16), z_shape, edge_shape, edge_shape),
        [pltpu.VMEM((8, 4 * LEAF, 4 * RANK), F32)],
    )(rhs, v_factor.reshape(leaves, 16, LANES), turn_col)
    z = exchange(z, COL)
    below, above = halos(low, high)
    step = 8
    near_wide = call(
        spread_near_kernel,
        [pl.BlockSpec((step, LANES, LANES), lambda i: (i, 0, 0))],
        shape((leaves // 2, LANES, 4 * LEAF), BF16),
        [pltpu.VMEM((step, LANES, LANES), F32), pltpu.VMEM((step, 2, LEAF, LANES), F32)],
        grid=(leaves // step,),
        out_specs=pl.BlockSpec((step // 2, LANES, 4 * LEAF), lambda i: (i, 0, 0)),
    )(near_rows)
    u_wide = call(
        spread_u_kernel,
        [VMEM],
        shape((groups, 4 * RANK, 4 * LEAF), BF16),
        [pltpu.VMEM((8, 2, 4 * RANK, LANES), F32)],
    )(u_factor.reshape(leaves, 16, LANES))
    t1 = exchange(first_mix(z), ROW)
    near_first = near(rhs, below, above)
    d, z, low, high = call(
        second_mix_kernel,
        [VMEM] * 5 + [SMEM],
        (field, z_shape, edge_shape, edge_shape),
        t2_scratch,
    )(t1, mix_second, u_wide, near_first, v_wide, turn_col)
    z = exchange(z, COL)
    below, above = halos(low, high)
    t1 = exchange(first_mix(z), ROW)
    near_second = near(d, below, above)
    e, sums = call(
        last_mix_kernel, [VMEM] * 6, (field, shape((devices, 8 * RHS), F32)), t2_scratch
    )(t1, mix_second, u_wide, near_second, rhs, d)
    sums = exchange(sums, ROW_COL)
    return call(finish_kernel, [VMEM] * 4, (field, field))(sums, rhs, d, e)


def solution(mesh):
    split = Mesh(mesh.devices.reshape(4, 2, 4, 4), ("row_0", "row_1", "col_0", "col_1"))
    return jax.shard_map(
        body,
        mesh=split,
        in_specs=(
            P(None, ROW_COL),
            P(ROW_COL, None, None),
            P(ROW_COL, None),
            P(ROW_COL, None),
            P(ROW, COL, None, None),
            P(ROW, COL, None, None),
            P(ROW_COL, None),
        ),
        out_specs=(P(None, ROW_COL), P(None, ROW_COL)),
        check_vma=False,
    )
```

time: 287 us -> 138 us (0.48); the launches traced: 282 us -> 137 us
  local copies, waits for them, and re-layouts: 91.4 us -> 8.5 us
  blocking collectives: 92.7 us -> 34 us
  Pallas kernels: 0 us -> 54.2 us
  matrix products: 36.4 us -> 0 us
  other arithmetic: 19.3 us -> 0.54 us
  starting transfers between devices: 41.1 us -> 38.2 us
    psum x12 -> x0, blocking collectives: 92.7 us -> none  [one_axis_at_a_time(): return functools.reduce(lax.psum, axes, x)]
    pallas_call x0 -> x10, Pallas kernels: none -> 54.2 us  [the longest x2 14.6 us: near(): call(near_kernel, [VMEM, VMEM, VMEM, SMEM, VMEM], field, [pltpu.VMEM((lea...]
    reshape x17 -> x0, local copies, waits for them, and re-layouts: 53.4 us -> none  [the longest x1 13 us: near_part(): blocks = near_blocks.reshape(leaves, blocks_per, LEAF, LEAF)]
    dot_general x10 -> x0, matrix products: 36.4 us -> none  [the longest x2 13.9 us: near_part(): jnp.einsum('slnu,lnvu->slv', picked, blocks, preferred_element_type=jnp.f...]
    all_to_all x0 -> x2, blocking collectives: none -> 34 us  [exchange(): return lax.all_to_all(x, axes, split_axis=0, concat_axis=0, tiled=True)]
    transpose x4 -> x0, local copies, waits for them, and re-layouts: 10.4 us -> none  [the longest x2 5.23 us: near_part(): jnp.einsum('slnu,lnvu->slv', picked, blocks, preferred_element_type=jnp.f...]
    gather x2 -> x0, local copies, waits for them, and re-layouts: 8.87 us -> none  [near_part(): picked = padded[:, position, :]]
    reduce_sum x4 -> x0, other arithmetic: 7.8 us -> none  [the longest x2 6.22 us: orthogonal(): jnp.sum(basis * image, axis=1)]
  transfers between devices with their start and end apart: 8 -> 7, of which waited for: 0 -> 1; matrix products, arithmetic and copies ran while one was open for 32% -> 1% of each run, Pallas kernels for 0% -> 24%
where the time goes in v1:
time: 138 us; the launch traced here: 137 us
  Pallas kernels  54.2 us (39%)
  starting transfers between devices  38.2 us (28%)
  blocking collectives  34 us (25%)
  local copies, waits for them, and re-layouts  8.5 us (6%)
    all_to_all x2, blocking collectives, exchange(): return lax.all_to_all(x, axes, split_axis=0, concat_axis=0, tiled=True)  34 us
    all_to_all x3, starting transfers between devices, exchange(): return lax.all_to_all(x, axes, split_axis=0, concat_axis=0, tiled=True)  19.5 us
    ppermute x4, starting transfers between devices, halos(): return (lax.ppermute(high, ROW_COL, up), lax.ppermute(low, ROW_COL, down))  18.7 us
    pallas_call x2, Pallas kernels, near(): call(near_kernel, [VMEM, VMEM, VMEM, SMEM, VMEM], field, [pltpu.VMEM((lea...  14.6 us
    pallas_call x1, Pallas kernels, body(): call(spread_near_kernel, [pl.BlockSpec((step, LANES, LANES), lambda i: (i...  11.7 us
    pallas_call x2, Pallas kernels, first_mix(): call(first_mix_kernel, [VMEM, VMEM, SMEM], shape((n_row, RHS, width_col),...  7.77 us
    unnamed x25, local copies, waits for them, and re-layouts  7.46 us
    pallas_call x1, Pallas kernels, body(): call(second_mix_kernel, [VMEM] * 5 + [SMEM], (field, z_shape, edge_shape,...  5.11 us
  transfers between devices with their start and end apart: 7, of which 1 were waited for; matrix products, arithmetic and copies ran while one was open for 1% of the time, Pallas kernels for 24%

profile of v1, /device:TPU:1, one launch (start us, length us, event | category | flops | bytes accessed | tf_op | source)
XLA Modules:
  0.0 136.9 jit_solution(2273061396953821061)
XLA Ops:
  0.6 0.0 copy-start.8
  0.7 0.0 copy-start.3
  0.7 2.0 %copy.13 = bf16[16,8,16,128]{3,2,1,0:T(8,128)(2,1)} copy(bf16[16,8,16,128]{3,1,2,0:T(8,128)(2,1)} %bitcast.27) | data formatting | bytes 1048576
  2.7 3.5 %spread_v_kernel.1 = (bf16[32,256,128]{2,1,0:T(8,128)(2,1)}, bf16[16,32,256]{2,1,0:T(8,128)(2,1)}, bf16[32,256]{1,0:T(8,128)(2,1)}, bf16[32,256]{1,0:T(8,128)(2,1)}) custom-call(f32[32,8192]{1,0:T(8,128)} %rhs_ref.5, bf16[128,16,128]{2,1,0:T(8,128)(2,1)} %bitcast.25, s32[1]{0:T(128)} %bitcast.turn_ref), custom_call_target="tpu_custom_call" | custom-call | flops 1000000 | bytes 1000000 | tf_op jit(solution)/shard_map/spread_v_kernel/pallas_call | solution.py:307
  6.2 8.6 %all-to-all-start = ((bf16[16,32,256]{2,1,0:T(8,128)(2,1)}), bf16[16,32,256]{2,1,0:T(8,128)(2,1)S(1)}, u32[]{:S(2)}, u32[]{:S(2)}) async-start(bf16[16,32,256]{2,1,0:T(8,128)(2,1)} %get-tuple-element.12), calls=%async_computation | async-start | bytes 524288 | tf_op jit(solution)/shard_map/all_to_all | solution.py:289
  14.8 3.3 %collective-permute-start = (bf16[32,256]{1,0:T(8,128)(2,1)}, bf16[32,256]{1,0:T(8,128)(2,1)S(1)}, u32[]{:S(2)}, u32[]{:S(2)}) collective-permute-start(bf16[32,256]{1,0:T(8,128)(2,1)} %get-tuple-element.13), channel_id=1, source_target_pairs={{0,1},{1,2},{2,3},{3,4},{4,5},{5,6},{6,7},{7,8},{8,9},{9,10},{10,1... | collective-permute-start | bytes 49160 | tf_op jit(solution)/shard_map/ppermute | solution.py:286
  18.0 6.4 %collective-permute-start.1 = (bf16[32,256]{1,0:T(8,128)(2,1)}, bf16[32,256]{1,0:T(8,128)(2,1)S(1)}, u32[]{:S(2)}, u32[]{:S(2)}) collective-permute-start(bf16[32,256]{1,0:T(8,128)(2,1)} %get-tuple-element.14), channel_id=1, source_target_pairs={{1,0},{2,1},{3,2},{4,3},{5,4},{6,5},{7,6},{8,7},{9,8},{10,9},{11,1... | collective-permute-start | bytes 49160 | tf_op jit(solution)/shard_map/ppermute | solution.py:286
  24.4 0.0 all-to-all-done.z_ref
  24.4 0.0 copy-start
  24.4 0.7 copy-done
  25.1 3.9 %first_mix_kernel.2 = bf16[8,32,512]{2,1,0:T(8,128)(2,1)} custom-call(bf16[16,32,256]{2,1,0:T(8,128)(2,1)} %copy-done, bf16[8,512,512]{2,1,0:T(8,128)(2,1)} %bitcast.19, s32[1]{0:T(128)} %bitcast.2.turn_ref), custom_call_target="tpu_custom_call" | custom-call | flops 1000000 | bytes 1000000 | tf_op jit(solution)/shard_map/first_mix_kernel/pallas_call | solution.py:300
  29.0 5.4 %all-to-all-start.1 = ((bf16[8,32,512]{2,1,0:T(8,128)(2,1)}), bf16[8,32,512]{2,1,0:T(8,128)(2,1)S(1)}, u32[]{:S(2)}, u32[]{:S(2)}) async-start(bf16[8,32,512]{2,1,0:T(8,128)(2,1)} %first_mix_kernel.2), calls=%async_computation.1 | async-start | bytes 524288 | tf_op jit(solution)/shard_map/all_to_all | solution.py:289
  34.4 0.0 copy-done.8
  34.4 0.5 add_bitcast_fusion.place_ref
  35.0 0.0 copy-done.3
  35.0 0.9 copy.14
  35.9 2.9 %spread_u_kernel.1.ubd_ref = bf16[32,128,256]{2,1,0:T(8,128)(2,1)} custom-call(bf16[128,16,128]{2,1,0:T(8,128)(2,1)} %bitcast.24), custom_call_target="tpu_custom_call" | custom-call | flops 1000000 | bytes 1000000 | tf_op jit(solution)/shard_map/spread_u_kernel/pallas_call | solution.py:324
  38.8 11.7 %spread_near_kernel.1.near_ref = bf16[64,128,256]{2,1,0:T(8,128)(2,1)} custom-call(bf16[128,128,128]{2,1,0:T(8,128)(2,1)} %bitcast.23), custom_call_target="tpu_custom_call" | custom-call | flops 1000000 | bytes 1000000 | tf_op jit(solution)/shard_map/spread_near_kernel/pallas_call | solution.py:316
  50.5 0.0 collective-permute-done.low_ref
  50.5 0.0 copy-start.4
  50.5 0.0 collective-permute-done.1.high_ref
  50.5 0.6 copy-done.4
  51.1 0.0 copy-start.5
  51.1 0.6 copy-done.5
  51.7 7.3 %near_kernel.2.near_ref = f32[32,8192]{1,0:T(8,128)} custom-call(f32[32,8192]{1,0:T(8,128)} %rhs_ref.5, bf16[32,256]{1,0:T(8,128)(2,1)} %copy-done.4, bf16[32,256]{1,0:T(8,128)(2,1)} %copy-done.5, s32[4,128]{1,0:T(4,128)} %add_bitcast_fusion.place_ref, bf16[64,128,256]{2,1,0:T(8,128)(2,1)} %spread_near_kernel.1.near_ref), custom_call_target="tpu_custom_call" | custom-call | flops 1000000 | bytes 1000000 | tf_op jit(solution)/shard_map/near_kernel/pallas_call | solution.py:292
  59.1 0.0 all-to-all-done.1.t1_ref
  59.1 0.0 copy-start.1
  59.1 0.7 copy-done.1
  59.8 5.1 %second_mix_kernel.1 = (f32[32,8192]{1,0:T(8,128)}, bf16[16,32,256]{2,1,0:T(8,128)(2,1)}, bf16[32,256]{1,0:T(8,128)(2,1)}, bf16[32,256]{1,0:T(8,128)(2,1)}) custom-call(bf16[8,32,512]{2,1,0:T(8,128)(2,1)} %copy-done.1, bf16[16,256,256]{2,1,0:T(8,128)(2,1)} %bitcast.21, bf16[32,128,256]{2,1,0:T(8,128)(2,1)} %spread_u_kernel.1.ubd_ref, ...), custom_call_target="tpu_custom_call" | custom-call | flops 1000000 | bytes 1000000 | tf_op jit(solution)/shard_map/second_mix_kernel/pallas_call | solution.py:332
  64.9 0.0 copy-start.10
  64.9 0.0 copy-start.9
  64.9 12.8 %all_to_all.31.z_ref = bf16[16,32,256]{2,1,0:T(8,128)(2,1)} all-to-all(bf16[16,32,256]{2,1,0:T(8,128)(2,1)} %get-tuple-element.16), channel_id=1, replica_groups=mesh['row_0'=4,'row_1'=2,'col_0'=4,'col_1'=4] {'col_0','col_1'}, dimensions={0} | all-to-all | bytes 524288 | tf_op jit(solution)/shard_map/all_to_all | solution.py:289
  77.7 3.9 %first_mix_kernel.3 = bf16[8,32,512]{2,1,0:T(8,128)(2,1)} custom-call(bf16[16,32,256]{2,1,0:T(8,128)(2,1)} %all_to_all.31.z_ref, bf16[8,512,512]{2,1,0:T(8,128)(2,1)} %bitcast.20, s32[1]{0:T(128)} %bitcast.2.turn_ref), custom_call_target="tpu_custom_call" | custom-call | flops 1000000 | bytes 1000000 | tf_op jit(solution)/shard_map/first_mix_kernel/pallas_call | solution.py:300
  81.6 5.5 %all-to-all-start.3 = ((bf16[8,32,512]{2,1,0:T(8,128)(2,1)}), bf16[8,32,512]{2,1,0:T(8,128)(2,1)S(1)}, u32[]{:S(2)}, u32[]{:S(2)}) async-start(bf16[8,32,512]{2,1,0:T(8,128)(2,1)} %first_mix_kernel.3), calls=%async_computation.3 | async-start | bytes 524288 | tf_op jit(solution)/shard_map/all_to_all | solution.py:289
  87.1 0.0 copy-done.10
  87.1 2.2 %collective-permute-start.2 = (bf16[32,256]{1,0:T(8,128)(2,1)S(1)}, bf16[32,256]{1,0:T(8,128)(2,1)S(1)}, u32[]{:S(2)}, u32[]{:S(2)}) collective-permute-start(bf16[32,256]{1,0:T(8,128)(2,1)S(1)} %copy-done.10), channel_id=1, source_target_pairs={{0,1},{1,2},{2,3},{3,4},{4,5},{5,6},{6,7},{7,8},{8,9},{9,10},{10,1... | collective-permute-start | bytes 49160 | tf_op jit(solution)/shard_map/ppermute | solution.py:286
  89.3 0.0 copy-done.9
  89.3 6.9 %collective-permute-start.3 = (bf16[32,256]{1,0:T(8,128)(2,1)S(1)}, bf16[32,256]{1,0:T(8,128)(2,1)S(1)}, u32[]{:S(2)}, u32[]{:S(2)}) collective-permute-start(bf16[32,256]{1,0:T(8,128)(2,1)S(1)} %copy-done.9), channel_id=1, source_target_pairs={{1,0},{2,1},{3,2},{4,3},{5,4},{6,5},{7,6},{8,7},{9,8},{10,9},{11,1... | collective-permute-start | bytes 49160 | tf_op jit(solution)/shard_map/ppermute | solution.py:286
  96.2 0.0 collective-permute-done.2.low_ref
  96.2 0.0 copy-start.6
  96.2 0.6 collective-permute-done.3.high_ref
  96.9 0.0 copy-start.7
  96.9 0.0 copy-done.6
  96.9 0.6 copy-done.7
  97.5 7.3 %near_kernel.3.near_ref = f32[32,8192]{1,0:T(8,128)} custom-call(f32[32,8192]{1,0:T(8,128)} %get-tuple-element.17.v_ref.d_ref, bf16[32,256]{1,0:T(8,128)(2,1)} %copy-done.6, bf16[32,256]{1,0:T(8,128)(2,1)} %copy-done.7, s32[4,128]{1,0:T(4,128)} %add_bitcast_fusion.place_ref, bf16[64,128,256]{2,1,0:T(8,128)(2,1)} %spread_near_kernel.1.near_ref), custom_call_target="tpu_custom_call" | custom-call | flops 1000000 | bytes 1000000 | tf_op jit(solution)/shard_map/near_kernel/pallas_call | solution.py:292
  104.8 0.0 all-to-all-done.3.t1_ref
  104.8 0.0 copy-start.2
  104.8 0.7 copy-done.2
  105.5 5.0 %last_mix_kernel.1 = (f32[32,8192]{1,0:T(8,128)}, f32[128,256]{1,0:T(8,128)}) custom-call(bf16[8,32,512]{2,1,0:T(8,128)(2,1)} %copy-done.2, bf16[16,256,256]{2,1,0:T(8,128)(2,1)} %bitcast.22, bf16[32,128,256]{2,1,0:T(8,128)(2,1)} %spread_u_kernel.1.ubd_ref, f32[32,8192]{1,0:T(8,128)} %near_kernel.3.near_ref, f32[32,8192]{1,0:T(8,128)} %rhs_ref.5, ...), custom_call_target="tpu_custom_call" | custom-call | flops 1000000 | bytes 1000000 | tf_op jit(solution)/shard_map/last_mix_kernel/pallas_call | solution.py:342
  110.6 1.0 copy.11
  111.6 21.2 %all_to_all.32 = f32[128,1,256]{2,1,0:T(1,128)S(1)} all-to-all(f32[128,1,256]{2,1,0:T(1,128)S(1)} %copy.11), channel_id=1, replica_groups=mesh['row_0'=4,'row_1'=2,'col_0'=4,'col_1'=4] {'row_0','row_1','col_0','..., dimensions={0} | all-to-all | bytes 262144 | tf_op jit(solution)/shard_map/all_to_all | solution.py:289
  132.8 0.6 copy.16
  133.4 3.5 %finish_kernel.1 = (f32[32,8192]{1,0:T(8,128)}, f32[32,8192]{1,0:T(8,128)}) custom-call(f32[128,256]{1,0:T(8,128)} %bitcast.26, f32[32,8192]{1,0:T(8,128)} %rhs_ref.5, f32[32,8192]{1,0:T(8,128)} %get-tuple-element.17.v_ref.d_ref, f32[32,8192]{1,0:T(8,128)} %get-tuple-element.21.e_ref), custom_call_target="tpu_custom_call" | custom-call | flops 1000000 | bytes 1000000 | tf_op jit(solution)/shard_map/finish_kernel/pallas_call | solution.py:346
  (1 shorter events, 0.0 us)
Async XLA Ops:
  0.6 33.8 %copy-start.8 = (s32[128,4]{0,1:T(4,128)S(1)}, s32[128,4]{0,1:T(4,128)}, u32[]{:S(2)}) copy-start(s32[128,4]{0,1:T(4,128)} %param.9) | copy-start | bytes 6148
  0.7 34.3 %copy-start.3 = (bf16[128,2048]{1,0:T(8,128)(2,1)S(1)}, bf16[128,2048]{1,0:T(8,128)(2,1)}, u32[]{:S(2)}) copy-start(bf16[128,2048]{1,0:T(8,128)(2,1)} %param.13) | copy-start | bytes 1572868
  6.2 18.3 %all-to-all-start = ((bf16[16,32,256]{2,1,0:T(8,128)(2,1)}), bf16[16,32,256]{2,1,0:T(8,128)(2,1)S(1)}, u32[]{:S(2)}, u32[]{:S(2)}) async-start(bf16[16,32,256]{2,1,0:T(8,128)(2,1)} %get-tuple-element.12), calls=%async_computation | async-start | bytes 524288 | tf_op jit(solution)/shard_map/all_to_all | solution.py:289
  14.8 35.8 %collective-permute-start = (bf16[32,256]{1,0:T(8,128)(2,1)}, bf16[32,256]{1,0:T(8,128)(2,1)S(1)}, u32[]{:S(2)}, u32[]{:S(2)}) collective-permute-start(bf16[32,256]{1,0:T(8,128)(2,1)} %get-tuple-element.13), channel_id=1, source_target_pairs={{0,1},{1,2},{2,3},{3,4},{4,5},{5,6},{6,7},{7,8},{8,9},{9,10},{10,1... | collective-permute-start | bytes 49160 | tf_op jit(solution)/shard_map/ppermute | solution.py:286
  18.0 32.5 %collective-permute-start.1 = (bf16[32,256]{1,0:T(8,128)(2,1)}, bf16[32,256]{1,0:T(8,128)(2,1)S(1)}, u32[]{:S(2)}, u32[]{:S(2)}) collective-permute-start(bf16[32,256]{1,0:T(8,128)(2,1)} %get-tuple-element.14), channel_id=1, source_target_pairs={{1,0},{2,1},{3,2},{4,3},{5,4},{6,5},{7,6},{8,7},{9,8},{10,9},{11,1... | collective-permute-start | bytes 49160 | tf_op jit(solution)/shard_map/ppermute | solution.py:286
  24.4 0.7 copy-start
  29.0 30.0 %all-to-all-start.1 = ((bf16[8,32,512]{2,1,0:T(8,128)(2,1)}), bf16[8,32,512]{2,1,0:T(8,128)(2,1)S(1)}, u32[]{:S(2)}, u32[]{:S(2)}) async-start(bf16[8,32,512]{2,1,0:T(8,128)(2,1)} %first_mix_kernel.2), calls=%async_computation.1 | async-start | bytes 524288 | tf_op jit(solution)/shard_map/all_to_all | solution.py:289
  50.5 0.6 copy-start.4
  51.1 0.6 copy-start.5
  59.1 0.7 copy-start.1
  64.9 22.3 %copy-start.10 = (bf16[32,256]{1,0:T(8,128)(2,1)S(1)}, bf16[32,256]{1,0:T(8,128)(2,1)}, u32[]{:S(2)}) copy-start(bf16[32,256]{1,0:T(8,128)(2,1)} %get-tuple-element.18) | copy-start | bytes 49156
  64.9 24.5 %copy-start.9 = (bf16[32,256]{1,0:T(8,128)(2,1)S(1)}, bf16[32,256]{1,0:T(8,128)(2,1)}, u32[]{:S(2)}) copy-start(bf16[32,256]{1,0:T(8,128)(2,1)} %get-tuple-element.19) | copy-start | bytes 49156
  81.6 23.2 %all-to-all-start.3 = ((bf16[8,32,512]{2,1,0:T(8,128)(2,1)}), bf16[8,32,512]{2,1,0:T(8,128)(2,1)S(1)}, u32[]{:S(2)}, u32[]{:S(2)}) async-start(bf16[8,32,512]{2,1,0:T(8,128)(2,1)} %first_mix_kernel.3), calls=%async_computation.3 | async-start | bytes 524288 | tf_op jit(solution)/shard_map/all_to_all | solution.py:289
  87.1 9.1 %collective-permute-start.2 = (bf16[32,256]{1,0:T(8,128)(2,1)S(1)}, bf16[32,256]{1,0:T(8,128)(2,1)S(1)}, u32[]{:S(2)}, u32[]{:S(2)}) collective-permute-start(bf16[32,256]{1,0:T(8,128)(2,1)S(1)} %copy-done.10), channel_id=1, source_target_pairs={{0,1},{1,2},{2,3},{3,4},{4,5},{5,6},{6,7},{7,8},{8,9},{9,10},{10,1... | collective-permute-start | bytes 49160 | tf_op jit(solution)/shard_map/ppermute | solution.py:286
  89.3 7.5 %collective-permute-start.3 = (bf16[32,256]{1,0:T(8,128)(2,1)S(1)}, bf16[32,256]{1,0:T(8,128)(2,1)S(1)}, u32[]{:S(2)}, u32[]{:S(2)}) collective-permute-start(bf16[32,256]{1,0:T(8,128)(2,1)S(1)} %copy-done.9), channel_id=1, source_target_pairs={{1,0},{2,1},{3,2},{4,3},{5,4},{6,5},{7,6},{8,7},{9,8},{10,9},{11,1... | collective-permute-start | bytes 49160 | tf_op jit(solution)/shard_map/ppermute | solution.py:286
  96.2 0.7 copy-start.6
  96.9 0.6 copy-start.7
  104.8 0.7 copy-start.2

commit v2 on v1

v2 whole, which is shorter than its diff:
```python
import jax
import jax.numpy as jnp
from jax import lax
from jax.experimental import pallas as pl
from jax.experimental.pallas import tpu as pltpu
from jax.sharding import Mesh
from jax.sharding import PartitionSpec as P

LEAF = 64
RANK = 32
HALO = 4
RHS = 32
LANES = 128
ROW_COL = ("row_0", "row_1", "col_0", "col_1")
ROW = ("row_0", "row_1")
COL = ("col_0", "col_1")
F32 = jnp.float32
BF16 = jnp.bfloat16


def dot(a, b):
    return jnp.dot(a, b, preferred_element_type=F32)


def dot_t(a, b):
    return lax.dot_general(a, b, (((1,), (1,)), ((), ())), preferred_element_type=F32)


def lane_group(rows):
    return lax.broadcasted_iota(jnp.int32, (rows, LANES), 1) // RANK


def lane_take(x, index):
    return jnp.take_along_axis(x, index, axis=1, mode="promise_in_bounds")


def lane_half(rows):
    return lax.broadcasted_iota(jnp.int32, (rows, LANES), 1) < LEAF


def pieces_of(source, target, sems, first, pieces, dim=0):
    size = source.shape[dim] // pieces
    at = [(slice(None),) * dim + (pl.ds(i * size, size),) for i in range(pieces)]
    return [pltpu.make_async_copy(source.at[x], target.at[x], sems.at[first + i]) for i, x in enumerate(at)]


class Queue:
    def __init__(self, copies, depth):
        self.copies, self.depth, self.done = copies, depth, 0
        for copy in copies[:depth]:
            copy.start()

    def wait(self, count=1):
        for _ in range(count):
            self.copies[self.done].wait()
            if self.done + self.depth < len(self.copies):
                self.copies[self.done + self.depth].start()
            self.done += 1


def wait_all(copies):
    for copy in copies:
        copy.wait()


def row_order(size, inner):
    row = lax.broadcasted_iota(jnp.int32, (size, size), 0)
    column = lax.broadcasted_iota(jnp.int32, (size, size), 1)
    outer = size // inner
    return jnp.where(column == row % outer * inner + row // outer, 1.0, 0.0).astype(BF16)


def leaf_rows(ref, sixteen, order):
    tiles = [ref[16 * sixteen : 16 * (sixteen + 1), t * LANES : (t + 1) * LANES] for t in range(16)]
    return dot(order, jnp.concatenate(tiles, axis=0))


def v_order():
    lane = lax.broadcasted_iota(jnp.int32, (RHS, LANES), 1)
    return lane // LEAF * LEAF + lane % 16 * 4 + lane % LEAF // 16


def compress(x, narrow, order, masks):
    lhs = jnp.concatenate([lane_take(x[:, t * LANES : (t + 1) * LANES], order).astype(BF16) for t in range(2)], axis=1)
    return dot(lhs, jnp.concatenate([narrow * mask for mask in masks], axis=0))


def group_masks(rows):
    group = lane_group(rows)
    return [jnp.where(group == leaf, 1.0, 0.0).astype(BF16) for leaf in range(4)]


def put_edges(v_ref, z_ref, place_ref):
    n_col, _, width = z_ref.shape
    edge = HALO * LEAF
    z_ref[lax.rem(place_ref[0] + 1, n_col), :, width - edge :] = v_ref[:, v_ref.shape[1] - edge :].astype(BF16)
    z_ref[lax.rem(place_ref[0] + n_col - 1, n_col), :, width - edge :] = v_ref[:, :edge].astype(BF16)


def spread_v_kernel(rhs_hbm, v_hbm, mix_hbm, turn_ref, vc_ref, z_ref, rhs_ref, mix_ref, v_ref, sems):
    mix_in = pieces_of(mix_hbm, mix_ref, sems, 8, 8)
    queue = Queue(pieces_of(v_hbm, v_ref, sems, 0, 4) + pieces_of(rhs_hbm, rhs_ref, sems, 4, 4, 1), 8)
    for copy in mix_in:
        copy.start()
    group = lane_group(16)
    shift = turn_ref[0] % 4 * RANK
    order = row_order(256, 16)
    groups = vc_ref.shape[0]
    for sixteen in range(groups // 4):
        if sixteen % (groups // 16) == 0:
            queue.wait()
        rows = leaf_rows(v_ref, sixteen, order)
        for h in range(4):
            of_leaf = [rows[16 * leaf : 16 * (leaf + 1)] for leaf in range(4 * h, 4 * h + 4)]
            for ur in range(4):
                x = of_leaf[ur]
                for leaf in range(4):
                    if leaf != ur:
                        x = jnp.where(group == leaf, pltpu.roll(of_leaf[leaf], (leaf - ur) * RANK % LANES, 1), x)
                vc_ref[4 * sixteen + h, 16 * ur : 16 * (ur + 1), :] = x.astype(BF16)
    masks = group_masks(LEAF)
    lanes = v_order()
    for g in range(groups):
        if g % (groups // 4) == 0:
            queue.wait()
        part = compress(rhs_ref[:, 256 * g : 256 * (g + 1)], vc_ref[g], lanes, masks)
        z_ref[g // 2, :, (g % 2) * LANES : (g % 2 + 1) * LANES] = pltpu.roll(part, shift, 1).astype(BF16)
    put_edges(rhs_ref, z_ref, turn_ref)
    wait_all(mix_in)


def spread_u(u_ref, uc_ref):
    half = lane_half(16)
    order = row_order(256, 16)
    for sixteen in range(uc_ref.shape[0] // 4):
        rows = leaf_rows(u_ref, sixteen, order)
        for h in range(4):
            for tile in range(2):
                leaf = 4 * h + 2 * tile
                a, b = rows[16 * leaf : 16 * (leaf + 1)], rows[16 * (leaf + 1) : 16 * (leaf + 2)]
                lanes = slice(tile * LANES, (tile + 1) * LANES)
                uc_ref[4 * sixteen + h, :16, lanes] = jnp.where(half, a, pltpu.roll(b, LEAF, 1)).astype(BF16)
                uc_ref[4 * sixteen + h, 16:, lanes] = jnp.where(half, pltpu.roll(a, LEAF, 1), b).astype(BF16)


def spread_near(near_ref, out_ref):
    half = lane_half(32)
    order = row_order(LANES, 4)
    for pair in range(out_ref.shape[0]):
        both = dot(order, jnp.concatenate([near_ref[2 * pair], near_ref[2 * pair + 1]], axis=1))
        for leaf in range(2):
            block = [both[32 * b : 32 * (b + 1), leaf * LANES : (leaf + 1) * LANES] for b in range(4)]
            for h in range(2):
                first, second = block[2 * h], block[2 * h + 1]
                even = jnp.where(half, first, pltpu.roll(second, LEAF, 1))
                odd = jnp.where(half, pltpu.roll(first, LEAF, 1), second)
                lanes = slice(h * LANES, (h + 1) * LANES)
                out_ref[pair, leaf * LEAF : leaf * LEAF + 32, lanes] = even.astype(BF16)
                out_ref[pair, leaf * LEAF + 32 : leaf * LEAF + 64, lanes] = odd.astype(BF16)


def near_kernel(v_ref, z_ref, t1_ref, turn_ref, place_ref, near_ref, out_ref, left, right):
    half = lane_half(RHS)
    lane = lax.broadcasted_iota(jnp.int32, (RHS, LANES), 1)
    order = lane // LEAF * LEAF + lane % 2 * 32 + lane % LEAF // 2
    edge = HALO // 2
    tiles = v_ref.shape[1] // LANES

    def put(t, x):
        turned = pltpu.roll(x, LEAF, 1)
        left[2 * t] = jnp.where(half, x, 0.0).astype(BF16)
        left[2 * t + 1] = jnp.where(half, turned, 0.0).astype(BF16)
        right[2 * t] = jnp.where(half, 0.0, turned).astype(BF16)
        right[2 * t + 1] = jnp.where(half, 0.0, x).astype(BF16)

    column, row = turn_ref[0], turn_ref[1]
    n_col, n_row = z_ref.shape[0], t1_ref.shape[0]
    z_lanes = slice(z_ref.shape[2] - HALO * LEAF, z_ref.shape[2])
    t1_lanes = slice(t1_ref.shape[2] - HALO * LEAF, t1_ref.shape[2])

    def beside(step, at_end, outside):
        near_by = z_ref[lax.clamp(0, column + step, n_col - 1), :, z_lanes].astype(F32)
        next_row = t1_ref[lax.clamp(0, row + step, n_row - 1), :, t1_lanes].astype(F32)
        return jnp.where(at_end, jnp.where(outside, 0.0, next_row), near_by)

    below = beside(-1, column == 0, row == 0)
    above = beside(1, column == n_col - 1, row == n_row - 1)
    for t in range(edge):
        put(t, below[:, t * LANES : (t + 1) * LANES])
        put(edge + tiles + t, above[:, t * LANES : (t + 1) * LANES])
    for t in range(tiles):
        put(edge + t, v_ref[:, t * LANES : (t + 1) * LANES])
    for pair in range(tiles):
        lhs = [
            jnp.concatenate(
                [left[place_ref[2 * h, leaf] + (leaf + HALO)] + right[place_ref[2 * h + 1, leaf] + (leaf + HALO)] for h in range(2)], axis=1
            )
            for leaf in (2 * pair, 2 * pair + 1)
        ]
        both = dot_t(jnp.concatenate(lhs, axis=0), near_ref[pair])
        out_ref[:, pair * LANES : (pair + 1) * LANES] = lane_take(jnp.where(half, both[:RHS], both[RHS:]), order)


def first_near_kernel(rows_ref, u_ref, v_ref, z_ref, t1_ref, turn_ref, place_ref, wide_ref, uc_ref, out_ref, left, right):
    spread_near(rows_ref, wide_ref)
    spread_u(u_ref, uc_ref)
    near_kernel(v_ref, z_ref, t1_ref, turn_ref, place_ref, wide_ref, out_ref, left, right)


def gather_lanes(parts, where_from, group):
    x = parts[(0 - where_from) % 4]
    for q in range(1, 4):
        x = jnp.where(group == q, parts[(q - where_from) % 4], x)
    return x


def turned_rows(ref_rows, count, where_from):
    order = [4 * four + (q - where_from) % 4 for four in range(count // 4) for q in range(4)]
    return jnp.concatenate([ref_rows[c * RANK : (c + 1) * RANK] for c in order], axis=0)


def first_mix_kernel(z_ref, mix_ref, turn_ref, out_ref):
    slots = mix_ref.shape[0]
    n_col = z_ref.shape[0]
    group = lane_group(RHS)
    shift = turn_ref[1] % 4 * RANK
    for j in range(slots):
        tile = j // 4
        lhs = jnp.concatenate(
            [
                gather_lanes(
                    [z_ref[4 * four + c, :, tile * LANES : (tile + 1) * LANES] for c in range(4)], j % 4, group
                )
                for four in range(n_col // 4)
            ],
            axis=1,
        )
        out = dot(lhs, turned_rows(mix_ref[j], n_col, j % 4))
        for t in range(out.shape[1] // LANES):
            out_ref[j, :, t * LANES : (t + 1) * LANES] = pltpu.roll(
                out[:, t * LANES : (t + 1) * LANES], shift, 1
            ).astype(BF16)
    first = turn_ref[0] == 0
    other_end = jnp.where(first, n_col - 1, 0)
    beside = lax.clamp(0, turn_ref[1] + jnp.where(first, 1, -1), slots - 1)
    edge = HALO * LEAF
    out_ref[beside, :, out_ref.shape[2] - edge :] = z_ref[other_end, :, z_ref.shape[2] - edge :]


def second_mix(t1_ref, mix_ref, t2_ref):
    n_row = t1_ref.shape[0]
    group = lane_group(RHS)
    count = mix_ref.shape[0]
    lane = lax.broadcasted_iota(jnp.int32, (RHS, LANES), 1)
    order = lane // RANK * RANK + lane % 16 * 2 + lane % RANK // 16
    for p in range(count):
        tile = p // 4
        lhs = jnp.concatenate(
            [
                gather_lanes(
                    [t1_ref[4 * four + r, :, tile * LANES : (tile + 1) * LANES] for r in range(4)], p % 4, group
                )
                for four in range(n_row // 4)
            ],
            axis=1,
        )
        out = dot(lhs, turned_rows(mix_ref[p], n_row, p % 4))
        for t in range(2):
            lanes = slice(t * LANES, (t + 1) * LANES)
            t2_ref[p, :, lanes] = lane_take(out[:, lanes], order).astype(BF16)


def expand_masks():
    lane = lax.broadcasted_iota(jnp.int32, (RANK, 2 * LANES), 1)
    return [jnp.where(lane // LEAF == leaf, 1.0, 0.0).astype(BF16) for leaf in range(4)]


def far_tile(t2_ref, uc_ref, masks, g):
    narrow = uc_ref[g]
    wide = jnp.concatenate([narrow * mask for mask in masks], axis=0)
    return dot(t2_ref[g // 2, :, (g % 2) * LANES : (g % 2 + 1) * LANES], wide)


def second_mix_kernel(
    t1_ref, mix_ref, uc_ref, near_ref, vc_ref, turn_ref, d_ref, z_ref, t2_ref
):
    second_mix(t1_ref, mix_ref, t2_ref)
    shift = turn_ref[0] % 4 * RANK
    groups = uc_ref.shape[0]
    masks = expand_masks()
    for g in range(groups):
        lanes = slice(256 * g, 256 * (g + 1))
        d_ref[:, lanes] = far_tile(t2_ref, uc_ref, masks, g) + near_ref[:, lanes]
    masks = group_masks(LEAF)
    order = v_order()
    for g in range(groups):
        part = compress(d_ref[:, 256 * g : 256 * (g + 1)], vc_ref[g], order, masks)
        z_ref[g // 2, :, (g % 2) * LANES : (g % 2 + 1) * LANES] = pltpu.roll(part, shift, 1).astype(BF16)
    put_edges(d_ref, z_ref, turn_ref)


def last_mix_kernel(t1_ref, mix_ref, uc_ref, near_ref, rhs_ref, d_ref, e_ref, sums_ref, t2_ref):
    second_mix(t1_ref, mix_ref, t2_ref)
    masks = expand_masks()
    total = [jnp.zeros((RHS, LANES), F32) for _ in range(6)]
    for g in range(uc_ref.shape[0]):
        wide = far_tile(t2_ref, uc_ref, masks, g) + near_ref[:, 256 * g : 256 * (g + 1)]
        e_ref[:, 256 * g : 256 * (g + 1)] = wide
        for t in range(2):
            lanes = slice(256 * g + LANES * t, 256 * g + LANES * (t + 1))
            r, d, e = rhs_ref[:, lanes], d_ref[:, lanes], wide[:, LANES * t : LANES * (t + 1)]
            terms = (r * r, r * d, d * d, r * e, d * e, e * e)
            total = [a + b for a, b in zip(total, terms)]
    stacked = jnp.concatenate(total + [jnp.zeros((2 * RHS, LANES), F32)], axis=0)
    row = jnp.sum(stacked.T, axis=0, keepdims=True)
    sums_ref[...] = jnp.broadcast_to(row[None], sums_ref.shape)


def finish_kernel(sums_ref, rhs_ref, d_ref, e_ref, solution_hbm, residual_hbm, solution_ref, residual_ref, sems):
    row = jnp.sum(sums_ref[...], axis=0)
    columns = jnp.broadcast_to(row, (LANES, row.shape[1])).T
    rr, rd, dd, re, de, ee = [columns[i * RHS : (i + 1) * RHS] for i in range(6)]
    scale = 1.0 / rr
    alpha = rd * scale
    h21_sq = (dd - alpha * rd) * scale
    h11 = 1.0 + alpha
    cross = re * scale - alpha * alpha
    inverse = 1.0 / h21_sq
    gain = ((de - alpha * dd - alpha * re + alpha * (alpha * rd)) * scale) * inverse
    h22 = 1.0 + gain
    spread = ((ee - 2.0 * alpha * de + alpha * (alpha * dd)) * scale) * inverse
    h32_sq = spread - gain * gain - cross * (cross * inverse)
    minor = h11 * h22 - cross
    determ = minor * minor + h32_sq * (h11 * h11 + h21_sq)
    x_first = (h22 * minor + h11 * h32_sq) / determ
    x_second = -minor / determ
    on_rhs = x_first - alpha * x_second
    on_d = x_first + x_second * (1.0 - alpha)
    solution_out = pieces_of(solution_ref, solution_hbm, sems, 0, 4, 1)
    residual_out = pieces_of(residual_ref, residual_hbm, sems, 4, 4, 1)
    tiles = rhs_ref.shape[1] // LANES
    for t in range(tiles):
        lanes = slice(t * LANES, (t + 1) * LANES)
        r, d, e = rhs_ref[:, lanes], d_ref[:, lanes], e_ref[:, lanes]
        solution_ref[:, lanes] = on_rhs * r + x_second * d
        residual_ref[:, lanes] = (1.0 - on_rhs) * r - on_d * d - x_second * e
        if (t + 1) % (tiles // 4) == 0:
            solution_out[t // (tiles // 4)].start()
            residual_out[t // (tiles // 4)].start()
    wait_all(solution_out + residual_out)


VMEM = pl.BlockSpec(memory_space=pltpu.VMEM)
HBM = pl.BlockSpec(memory_space=pltpu.HBM)
SMEM = pl.BlockSpec(memory_space=pltpu.SMEM)
MIB = 1 << 20
KEPT = pltpu.VMEM
FAR_OFF = pltpu.HBM


def call(kernel, in_specs, outs, scratch=(), sems=0, limit=8):
    run = pl.pallas_call(
        kernel,
        in_specs=in_specs,
        out_shape=[space(dims, dtype) for space, dims, dtype, _ in outs],
        out_specs=[spec for *_, spec in outs],
        scratch_shapes=[pltpu.VMEM(*x) for x in scratch] + [pltpu.SemaphoreType.DMA((sems,))] * (sems > 0),
        cost_estimate=pl.CostEstimate(flops=1_000_000, bytes_accessed=1_000_000, transcendentals=0),
        compiler_params=pltpu.CompilerParams(vmem_limit_bytes=limit * MIB),
        name=kernel.__name__,
    )

    def placed(*args):
        spaces = {id(VMEM): pltpu.VMEM, id(HBM): pltpu.HBM}
        args = [
            pltpu.with_memory_space_constraint(x, spaces[id(spec)]) if id(spec) in spaces else x
            for x, spec in zip(args, in_specs)
        ]
        out = run(*args)
        return out if len(outs) > 1 else out[0]

    return placed


def body(rhs, near_blocks, near_offsets, v_factor, mix_col, mix_row, u_factor):
    count = rhs.shape[1]
    leaves = near_offsets.shape[0]
    n_row = lax.axis_size(ROW)
    n_col = lax.axis_size(COL)
    devices = n_row * n_col
    slots = leaves // n_col
    groups = leaves // 4
    width_col = n_col * RANK
    width_row = n_row * RANK
    turn = jnp.stack([lax.axis_index(COL), lax.axis_index(ROW)]).astype(jnp.int32)
    place = near_offsets.T
    near_rows = (
        near_blocks.reshape(leaves, 4, 32, LANES).transpose(0, 2, 1, 3).reshape(leaves, LANES, LANES)
    )
    mix_first = mix_col.reshape(slots, width_col, width_col)
    mix_second = mix_row.reshape(n_col, width_row, width_row)
    field = ((RHS, count), F32)
    vc_shape = ((groups, LEAF, LANES), BF16)
    uc_shape = ((groups, RANK, 2 * LANES), BF16)
    wide_shape = ((leaves // 2, LANES, 4 * LEAF), BF16)
    z_out = (KEPT, (n_col, RHS, slots * RANK + HALO * LEAF), BF16, VMEM)
    t1_out = (KEPT, (n_row, RHS, width_col + HALO * LEAF), BF16, VMEM)
    t2_shape = ((n_col, RHS, width_row), BF16)

    def exchange(x, axes):
        return lax.all_to_all(x, axes, split_axis=0, concat_axis=0, tiled=True)

    store = ((leaves + 2 * HALO, RHS, LANES), BF16)

    vc, z, rhs_kept, mix_kept = call(
        spread_v_kernel,
        [HBM, HBM, HBM, SMEM],
        [(KEPT, *vc_shape, VMEM), z_out, (KEPT, *field, VMEM), (KEPT, mix_first.shape, BF16, VMEM)],
        [(v_factor.shape, BF16)],
        16,
    )(rhs, v_factor, mix_first, turn)

    def first_mix(z):
        return call(first_mix_kernel, [VMEM, VMEM, SMEM], [t1_out])(z, mix_kept, turn)

    z = exchange(z, COL)
    t1 = exchange(first_mix(z), ROW)
    t1, place = lax.optimization_barrier((t1, place))
    near_wide, uc, near_first = call(
        first_near_kernel,
        [VMEM, VMEM, VMEM, VMEM, VMEM, SMEM, SMEM],
        [(KEPT, *wide_shape, VMEM), (KEPT, *uc_shape, VMEM), (KEPT, *field, VMEM)],
        [store, store],
    )(near_rows, u_factor, rhs_kept, z, t1, turn, place)
    d, z = call(
        second_mix_kernel, [VMEM] * 5 + [SMEM], [(KEPT, *field, VMEM), z_out], [t2_shape]
    )(t1, mix_second, uc, near_first, vc, turn)
    z = exchange(z, COL)
    t1 = exchange(first_mix(z), ROW)
    near_second = call(
        near_kernel, [VMEM, VMEM, VMEM, SMEM, SMEM, VMEM], [(KEPT, *field, VMEM)], [store, store]
    )(d, z, t1, turn, place, near_wide)
    e, sums = call(
        last_mix_kernel,
        [VMEM] * 6,
        [(KEPT, *field, VMEM), (KEPT, (devices, 1, 8 * RHS), F32, VMEM)],
        [t2_shape],
    )(t1, mix_second, uc, near_second, rhs_kept, d)
    sums = exchange(sums, ROW_COL)
    return tuple(
        call(
            finish_kernel, [VMEM] * 4, [(FAR_OFF, *field, HBM)] * 2, [field, field], 8
        )(sums, rhs_kept, d, e)
    )


def solution(mesh):
    split = Mesh(mesh.devices.reshape(4, 2, 4, 4), ("row_0", "row_1", "col_0", "col_1"))
    return jax.shard_map(
        body,
        mesh=split,
        in_specs=(
            P(None, ROW_COL),
            P(ROW_COL, None, None),
            P(ROW_COL, None),
            P(ROW_COL, None),
            P(ROW, COL, None, None),
            P(ROW, COL, None, None),
            P(ROW_COL, None),
        ),
        out_specs=(P(None, ROW_COL), P(None, ROW_COL)),
        check_vma=False,
    )
```

time: 138 us -> 93.1 us (0.67)
  blocking collectives: 34 us -> 73.3 us
  starting transfers between devices: 38.2 us -> 0 us
  Pallas kernels: 54.2 us -> 18.6 us
  local copies, waits for them, and re-layouts: 8.5 us -> 0.03 us
    all_to_all x2 -> x5, blocking collectives: 34 us -> 73.3 us  [exchange(): return lax.all_to_all(x, axes, split_axis=0, concat_axis=0, tiled=True)]
    pallas_call x10 -> x8, Pallas kernels: 54.2 us -> 18.6 us  [placed(): out = run(*args)]
    all_to_all x3 -> x0, starting transfers between devices: 19.5 us -> none  [exchange(): return lax.all_to_all(x, axes, split_axis=0, concat_axis=0, tiled=True)]
    ppermute x4 -> x0, starting transfers between devices: 18.7 us -> none  [halos(): return (lax.ppermute(high, ROW_COL, up), lax.ppermute(low, ROW_COL, down))]
    unnamed x25 -> x8, local copies, waits for them, and re-layouts: 7.46 us -> 0.03 us
  transfers between devices with their start and end apart: 7 -> 0, of which waited for: 1 -> 0; matrix products, arithmetic and copies ran while one was open for 1% -> 0% of each run, Pallas kernels for 24% -> 0%
where the time goes in v2:
time: 93.1 us; the launch traced here: 92.8 us
  blocking collectives  73.3 us (79%)
  Pallas kernels  18.6 us (20%)
    all_to_all x5, blocking collectives, exchange(): return lax.all_to_all(x, axes, split_axis=0, concat_axis=0, tiled=True)  73.3 us
    pallas_call x8, Pallas kernels, placed(): out = run(*args)  18.6 us

profile of v2, /device:TPU:1, one launch (start us, length us, event | category | flops | bytes accessed | tf_op | source)
XLA Modules:
  0.0 92.8 jit_solution(6715246856625691655)
XLA Ops:
  0.6 0.1 pad_add_fusion.turn_ref
  0.7 4.2 %spread_v_kernel.1 = (bf16[32,64,128]{2,1,0:T(8,128)(2,1)S(1)}, bf16[16,32,512]{2,1,0:T(8,128)(2,1)S(1)}, f32[32,8192]{1,0:T(8,128)S(1)}, bf16[8,512,512]{2,1,0:T(8,128)(2,1)S(1)}) custom-call(f32[32,8192]{1,0:T(8,128)} %rhs_hbm.1, bf16[128,2048]{1,0:T(8,128)(2,1)} %v_hbm.1, bf16[8,512,512]{2,1,0:T(8,128)(2,1)} %bitcast.15, s32[2]{0:T(128)S(1)} %pad_add_fusion.turn_ref), custom_call_target="tpu_custom_call" | custom-call | flops 1000000 | bytes 1000000 | tf_op jit(solution)/shard_map/spread_v_kernel/pallas_call | solution.py:379
  4.9 0.0 copy-start.1
  5.0 0.0 copy-start.2
  5.0 0.0 copy-start.3
  5.0 19.1 %all_to_all.25.z_ref = bf16[16,32,512]{2,1,0:T(8,128)(2,1)S(1)} all-to-all(bf16[16,32,512]{2,1,0:T(8,128)(2,1)S(1)} %get-tuple-element.15), channel_id=1, replica_groups=mesh['row_0'=4,'row_1'=2,'col_0'=4,'col_1'=4] {'col_0','col_1'}, dimensions={0} | all-to-all | bytes 1048576 | tf_op jit(solution)/shard_map/all_to_all | solution.py:411
  24.1 1.5 %first_mix_kernel.2 = bf16[8,32,768]{2,1,0:T(8,128)(2,1)S(1)} custom-call(bf16[16,32,512]{2,1,0:T(8,128)(2,1)S(1)} %all_to_all.25.z_ref, bf16[8,512,512]{2,1,0:T(8,128)(2,1)S(1)} %get-tuple-element.16.mix_ref, s32[2]{0:T(128)S(1)} %pad_add_fusion.turn_ref), custom_call_target="tpu_custom_call" | custom-call | flops 1000000 | bytes 1000000 | tf_op jit(solution)/shard_map/first_mix_kernel/pallas_call | solution.py:379
  25.5 0.0 copy-start
  25.5 14.4 %all_to_all.26.t1_ref = bf16[8,32,768]{2,1,0:T(8,128)(2,1)S(1)} all-to-all(bf16[8,32,768]{2,1,0:T(8,128)(2,1)S(1)} %first_mix_kernel.2), channel_id=1, replica_groups=mesh['row_0'=4,'row_1'=2,'col_0'=4,'col_1'=4] {'row_0','row_1'}, dimensions={0} | all-to-all | bytes 786432 | tf_op jit(solution)/shard_map/all_to_all | solution.py:411
  39.9 0.0 copy-done.1
  39.9 0.0 copy-done.2
  39.9 0.0 copy-done.3
  39.9 4.3 %first_near_kernel.1 = (bf16[64,128,256]{2,1,0:T(8,128)(2,1)S(1)}, bf16[32,32,256]{2,1,0:T(8,128)(2,1)S(1)}, f32[32,8192]{1,0:T(8,128)S(1)}) custom-call(bf16[128,128,128]{2,1,0:T(8,128)(2,1)S(1)} %bitcast.12, bf16[128,2048]{1,0:T(8,128)(2,1)S(1)} %copy-done.2, f32[32,8192]{1,0:T(8,128)S(1)} %get-tuple-element.18.v_ref.rhs_ref, ...), custom_call_target="tpu_custom_call" | custom-call | flops 1000000 | bytes 1000000 | tf_op jit(solution)/shard_map/first_near_kernel/pallas_call | solution.py:379
  44.2 0.0 copy-done
  44.2 1.7 %second_mix_kernel.1 = (f32[32,8192]{1,0:T(8,128)S(1)}, bf16[16,32,512]{2,1,0:T(8,128)(2,1)S(1)}) custom-call(bf16[8,32,768]{2,1,0:T(8,128)(2,1)S(1)} %all_to_all.26.t1_ref, bf16[16,256,256]{2,1,0:T(8,128)(2,1)S(1)} %bitcast.10, bf16[32,32,256]{2,1,0:T(8,128)(2,1)S(1)} %get-tuple-element.20.uc_ref, f32[32,8192]{1,0:T(8,128)S(1)} %get-tuple-element.21.near_ref, ...), custom_call_target="tpu_custom_call" | custom-call | flops 1000000 | bytes 1000000 | tf_op jit(solution)/shard_map/second_mix_kernel/pallas_call | solution.py:379
  45.9 13.2 %all_to_all.27.z_ref = bf16[16,32,512]{2,1,0:T(8,128)(2,1)S(1)} all-to-all(bf16[16,32,512]{2,1,0:T(8,128)(2,1)S(1)} %get-tuple-element.23), channel_id=1, replica_groups=mesh['row_0'=4,'row_1'=2,'col_0'=4,'col_1'=4] {'col_0','col_1'}, dimensions={0} | all-to-all | bytes 1048576 | tf_op jit(solution)/shard_map/all_to_all | solution.py:411
  59.1 1.4 %first_mix_kernel.3 = bf16[8,32,768]{2,1,0:T(8,128)(2,1)S(1)} custom-call(bf16[16,32,512]{2,1,0:T(8,128)(2,1)S(1)} %all_to_all.27.z_ref, bf16[8,512,512]{2,1,0:T(8,128)(2,1)S(1)} %get-tuple-element.16.mix_ref, s32[2]{0:T(128)S(1)} %pad_add_fusion.turn_ref), custom_call_target="tpu_custom_call" | custom-call | flops 1000000 | bytes 1000000 | tf_op jit(solution)/shard_map/first_mix_kernel/pallas_call | solution.py:379
  60.6 12.4 %all_to_all.28.t1_ref = bf16[8,32,768]{2,1,0:T(8,128)(2,1)S(1)} all-to-all(bf16[8,32,768]{2,1,0:T(8,128)(2,1)S(1)} %first_mix_kernel.3), channel_id=1, replica_groups=mesh['row_0'=4,'row_1'=2,'col_0'=4,'col_1'=4] {'row_0','row_1'}, dimensions={0} | all-to-all | bytes 786432 | tf_op jit(solution)/shard_map/all_to_all | solution.py:411
  73.0 2.5 %near_kernel.1.near_ref = f32[32,8192]{1,0:T(8,128)S(1)} custom-call(f32[32,8192]{1,0:T(8,128)S(1)} %get-tuple-element.24.v_ref.d_ref, bf16[16,32,512]{2,1,0:T(8,128)(2,1)S(1)} %all_to_all.27.z_ref, bf16[8,32,768]{2,1,0:T(8,128)(2,1)S(1)} %all_to_all.28.t1_ref, s32[2]{0:T(128)S(1)} %pad_add_fusion.turn_ref, s32[4,128]{1,0:T(4,128)S(1)} %bitcast.14, ...), custom_call_target="tpu_custom_call" | custom-call | flops 1000000 | bytes 1000000 | tf_op jit(solution)/shard_map/near_kernel/pallas_call | solution.py:379
  75.5 1.3 %last_mix_kernel.1 = (f32[32,8192]{1,0:T(8,128)S(1)}, f32[128,1,256]{2,1,0:T(1,128)S(1)}) custom-call(bf16[8,32,768]{2,1,0:T(8,128)(2,1)S(1)} %all_to_all.28.t1_ref, bf16[16,256,256]{2,1,0:T(8,128)(2,1)S(1)} %bitcast.11, bf16[32,32,256]{2,1,0:T(8,128)(2,1)S(1)} %get-tuple-element.20.uc_ref, f32[32,8192]{1,0:T(8,128)S(1)} %near_kernel.1.near_ref, ...), custom_call_target="tpu_custom_call" | custom-call | flops 1000000 | bytes 1000000 | tf_op jit(solution)/shard_map/last_mix_kernel/pallas_call | solution.py:379
  76.8 14.3 %all_to_all.29.sums_ref = f32[128,1,256]{2,1,0:T(1,128)S(1)} all-to-all(f32[128,1,256]{2,1,0:T(1,128)S(1)} %get-tuple-element.26), channel_id=1, replica_groups=mesh['row_0'=4,'row_1'=2,'col_0'=4,'col_1'=4] {'row_0','row_1','col_0','..., dimensions={0} | all-to-all | bytes 262144 | tf_op jit(solution)/shard_map/all_to_all | solution.py:411
  91.1 1.7 %finish_kernel.1 = (f32[32,8192]{1,0:T(8,128)}, f32[32,8192]{1,0:T(8,128)}) custom-call(f32[128,1,256]{2,1,0:T(1,128)S(1)} %all_to_all.29.sums_ref, f32[32,8192]{1,0:T(8,128)S(1)} %get-tuple-element.18.v_ref.rhs_ref, f32[32,8192]{1,0:T(8,128)S(1)} %get-tuple-element.24.v_ref.d_ref, f32[32,8192]{1,0:T(8,128)S(1)} %get-tuple-element.27.e_ref), custom_call_target="tpu_custom_call" | custom-call | flops 1000000 | bytes 1000000 | tf_op jit(solution)/shard_map/finish_kernel/pallas_call | solution.py:379
Async XLA Ops:
  4.9 34.9 %copy-start.1 = (bf16[128,4,4096]{2,1,0:T(4,128)(2,1)S(1)}, bf16[128,4,4096]{2,1,0:T(4,128)(2,1)}, u32[]{:S(2)}) copy-start(bf16[128,4,4096]{2,1,0:T(4,128)(2,1)} %param.8) | copy-start | bytes 12582916
  5.0 34.9 %copy-start.2 = (bf16[128,2048]{1,0:T(8,128)(2,1)S(1)}, bf16[128,2048]{1,0:T(8,128)(2,1)}, u32[]{:S(2)}) copy-start(bf16[128,2048]{1,0:T(8,128)(2,1)} %u_ref.1) | copy-start | bytes 1572868
  5.0 34.9 %copy-start.3 = (s32[128,4]{0,1:T(4,128)S(1)}, s32[128,4]{0,1:T(4,128)}, u32[]{:S(2)}) copy-start(s32[128,4]{0,1:T(4,128)} %param.9) | copy-start | bytes 6148
  25.5 18.6 %copy-start = (bf16[1,16,256,256]{3,2,1,0:T(8,128)(2,1)S(1)}, bf16[1,16,256,256]{3,2,1,0:T(8,128)(2,1)}, u32[]{:S(2)}) copy-start(bf16[1,16,256,256]{3,2,1,0:T(8,128)(2,1)} %param.12) | copy-start | bytes 6291460

commit v3 on v2

--- a/solution.py
+++ b/solution.py
@@ -38,6 +38,14 @@
     return lax.broadcasted_iota(jnp.int32, (rows, LANES), 1) < LEAF
 
 
+def column_index():
+    return lax.axis_index("col_0") * lax.axis_size("col_1") + lax.axis_index("col_1")
+
+
+def row_index():
+    return lax.axis_index("row_0") * lax.axis_size("row_1") + lax.axis_index("row_1")
+
+
 def pieces_of(source, target, sems, first, pieces, dim=0):
     size = source.shape[dim] // pieces
     at = [(slice(None),) * dim + (pl.ds(i * size, size),) for i in range(pieces)]
@@ -90,20 +98,20 @@
     return [jnp.where(group == leaf, 1.0, 0.0).astype(BF16) for leaf in range(4)]
 
 
-def put_edges(v_ref, z_ref, place_ref):
+def put_edges(v_ref, z_ref):
     n_col, _, width = z_ref.shape
     edge = HALO * LEAF
-    z_ref[lax.rem(place_ref[0] + 1, n_col), :, width - edge :] = v_ref[:, v_ref.shape[1] - edge :].astype(BF16)
-    z_ref[lax.rem(place_ref[0] + n_col - 1, n_col), :, width - edge :] = v_ref[:, :edge].astype(BF16)
-
-
-def spread_v_kernel(rhs_hbm, v_hbm, mix_hbm, turn_ref, vc_ref, z_ref, rhs_ref, mix_ref, v_ref, sems):
+    z_ref[lax.rem(column_index() + 1, n_col), :, width - edge :] = v_ref[:, v_ref.shape[1] - edge :].astype(BF16)
+    z_ref[lax.rem(column_index() + n_col - 1, n_col), :, width - edge :] = v_ref[:, :edge].astype(BF16)
+
+
+def spread_v_kernel(rhs_hbm, v_hbm, mix_hbm, vc_ref, z_ref, rhs_ref, mix_ref, v_ref, sems):
+    queue = Queue(pieces_of(v_hbm, v_ref, sems, 0, 4) + pieces_of(rhs_hbm, rhs_ref, sems, 4, 4, 1), 8)
     mix_in = pieces_of(mix_hbm, mix_ref, sems, 8, 8)
-    queue = Queue(pieces_of(v_hbm, v_ref, sems, 0, 4) + pieces_of(rhs_hbm, rhs_ref, sems, 4, 4, 1), 8)
     for copy in mix_in:
         copy.start()
     group = lane_group(16)
-    shift = turn_ref[0] % 4 * RANK
+    shift = column_index() % 4 * RANK
     order = row_order(256, 16)
     groups = vc_ref.shape[0]
     for sixteen in range(groups // 4):
@@ -125,7 +133,7 @@
             queue.wait()
         part = compress(rhs_ref[:, 256 * g : 256 * (g + 1)], vc_ref[g], lanes, masks)
         z_ref[g // 2, :, (g % 2) * LANES : (g % 2 + 1) * LANES] = pltpu.roll(part, shift, 1).astype(BF16)
-    put_edges(rhs_ref, z_ref, turn_ref)
+    put_edges(rhs_ref, z_ref)
     wait_all(mix_in)
 
 
@@ -159,7 +167,7 @@
                 out_ref[pair, leaf * LEAF + 32 : leaf * LEAF + 64, lanes] = odd.astype(BF16)
 
 
-def near_kernel(v_ref, z_ref, t1_ref, turn_ref, place_ref, near_ref, out_ref, left, right):
+def near_product(v_ref, z_ref, t1_ref, place_ref, near_ref, out_ref, left, right, table):
     half = lane_half(RHS)
     lane = lax.broadcasted_iota(jnp.int32, (RHS, LANES), 1)
     order = lane // LEAF * LEAF + lane % 2 * 32 + lane % LEAF // 2
@@ -173,7 +181,7 @@
         right[2 * t] = jnp.where(half, 0.0, turned).astype(BF16)
         right[2 * t + 1] = jnp.where(half, 0.0, x).astype(BF16)
 
-    column, row = turn_ref[0], turn_ref[1]
+    column, row = column_index(), row_index()
     n_col, n_row = z_ref.shape[0], t1_ref.shape[0]
     z_lanes = slice(z_ref.shape[2] - HALO * LEAF, z_ref.shape[2])
     t1_lanes = slice(t1_ref.shape[2] - HALO * LEAF, t1_ref.shape[2])
@@ -190,6 +198,7 @@
         put(edge + tiles + t, above[:, t * LANES : (t + 1) * LANES])
     for t in range(tiles):
         put(edge + t, v_ref[:, t * LANES : (t + 1) * LANES])
+    table.wait()
     for pair in range(tiles):
         lhs = [
             jnp.concatenate(
@@ -201,12 +210,6 @@
         out_ref[:, pair * LANES : (pair + 1) * LANES] = lane_take(jnp.where(half, both[:RHS], both[RHS:]), order)
 
 
-def first_near_kernel(rows_ref, u_ref, v_ref, z_ref, t1_ref, turn_ref, place_ref, wide_ref, uc_ref, out_ref, left, right):
-    spread_near(rows_ref, wide_ref)
-    spread_u(u_ref, uc_ref)
-    near_kernel(v_ref, z_ref, t1_ref, turn_ref, place_ref, wide_ref, out_ref, left, right)
-
-
 def gather_lanes(parts, where_from, group):
     x = parts[(0 - where_from) % 4]
     for q in range(1, 4):
@@ -219,11 +222,11 @@
     return jnp.concatenate([ref_rows[c * RANK : (c + 1) * RANK] for c in order], axis=0)
 
 
-def first_mix_kernel(z_ref, mix_ref, turn_ref, out_ref):
+def first_mix_kernel(z_ref, mix_ref, out_ref):
     slots = mix_ref.shape[0]
     n_col = z_ref.shape[0]
     group = lane_group(RHS)
-    shift = turn_ref[1] % 4 * RANK
+    shift = row_index() % 4 * RANK
     for j in range(slots):
         tile = j // 4
         lhs = jnp.concatenate(
@@ -240,9 +243,9 @@
             out_ref[j, :, t * LANES : (t + 1) * LANES] = pltpu.roll(
                 out[:, t * LANES : (t + 1) * LANES], shift, 1
             ).astype(BF16)
-    first = turn_ref[0] == 0
+    first = column_index() == 0
     other_end = jnp.where(first, n_col - 1, 0)
-    beside = lax.clamp(0, turn_ref[1] + jnp.where(first, 1, -1), slots - 1)
+    beside = lax.clamp(0, row_index() + jnp.where(first, 1, -1), slots - 1)
     edge = HALO * LEAF
     out_ref[beside, :, out_ref.shape[2] - edge :] = z_ref[other_end, :, z_ref.shape[2] - edge :]
 
@@ -281,11 +284,18 @@
     return dot(t2_ref[g // 2, :, (g % 2) * LANES : (g % 2 + 1) * LANES], wide)
 
 
-def second_mix_kernel(
-    t1_ref, mix_ref, uc_ref, near_ref, vc_ref, turn_ref, d_ref, z_ref, t2_ref
+def first_apply_kernel(
+    rows_ref, u_ref, v_ref, in_ref, t1_ref, place_hbm, mix_ref, vc_ref,
+    wide_ref, uc_ref, d_ref, z_ref,
+    near_ref, left, right, t2_ref, place_ref, sem,
 ):
+    table = pltpu.make_async_copy(place_hbm, place_ref, sem)
+    table.start()
+    spread_near(rows_ref, wide_ref)
+    spread_u(u_ref, uc_ref)
     second_mix(t1_ref, mix_ref, t2_ref)
-    shift = turn_ref[0] % 4 * RANK
+    near_product(v_ref, in_ref, t1_ref, place_ref, wide_ref, near_ref, left, right, table)
+    shift = column_index() % 4 * RANK
     groups = uc_ref.shape[0]
     masks = expand_masks()
     for g in range(groups):
@@ -296,11 +306,18 @@
     for g in range(groups):
         part = compress(d_ref[:, 256 * g : 256 * (g + 1)], vc_ref[g], order, masks)
         z_ref[g // 2, :, (g % 2) * LANES : (g % 2 + 1) * LANES] = pltpu.roll(part, shift, 1).astype(BF16)
-    put_edges(d_ref, z_ref, turn_ref)
-
-
-def last_mix_kernel(t1_ref, mix_ref, uc_ref, near_ref, rhs_ref, d_ref, e_ref, sums_ref, t2_ref):
+    put_edges(d_ref, z_ref)
+
+
+def second_apply_kernel(
+    t1_ref, mix_ref, uc_ref, wide_ref, in_ref, place_hbm, rhs_ref, d_ref,
+    e_ref, sums_ref,
+    near_ref, left, right, t2_ref, place_ref, sem,
+):
+    table = pltpu.make_async_copy(place_hbm, place_ref, sem)
+    table.start()
     second_mix(t1_ref, mix_ref, t2_ref)
+    near_product(d_ref, in_ref, t1_ref, place_ref, wide_ref, near_ref, left, right, table)
     masks = expand_masks()
     total = [jnp.zeros((RHS, LANES), F32) for _ in range(6)]
     for g in range(uc_ref.shape[0]):
@@ -358,13 +375,15 @@
 FAR_OFF = pltpu.HBM
 
 
-def call(kernel, in_specs, outs, scratch=(), sems=0, limit=8):
+def call(kernel, in_specs, outs, scratch=(), sems=0, limit=8, table=None):
     run = pl.pallas_call(
         kernel,
         in_specs=in_specs,
         out_shape=[space(dims, dtype) for space, dims, dtype, _ in outs],
         out_specs=[spec for *_, spec in outs],
-        scratch_shapes=[pltpu.VMEM(*x) for x in scratch] + [pltpu.SemaphoreType.DMA((sems,))] * (sems > 0),
+        scratch_shapes=[pltpu.VMEM(*x) for x in scratch]
+        + [pltpu.SemaphoreType.DMA((sems,))] * (sems > 0)
+        + ([] if table is None else [pltpu.SMEM(table.shape, table.dtype), pltpu.SemaphoreType.DMA]),
         cost_estimate=pl.CostEstimate(flops=1_000_000, bytes_accessed=1_000_000, transcendentals=0),
         compiler_params=pltpu.CompilerParams(vmem_limit_bytes=limit * MIB),
         name=kernel.__name__,
@@ -392,7 +411,6 @@
     groups = leaves // 4
     width_col = n_col * RANK
     width_row = n_row * RANK
-    turn = jnp.stack([lax.axis_index(COL), lax.axis_index(ROW)]).astype(jnp.int32)
     place = near_offsets.T
     near_rows = (
         near_blocks.reshape(leaves, 4, 32, LANES).transpose(0, 2, 1, 3).reshape(leaves, LANES, LANES)
@@ -414,38 +432,34 @@
 
     vc, z, rhs_kept, mix_kept = call(
         spread_v_kernel,
-        [HBM, HBM, HBM, SMEM],
+        [HBM, HBM, HBM],
         [(KEPT, *vc_shape, VMEM), z_out, (KEPT, *field, VMEM), (KEPT, mix_first.shape, BF16, VMEM)],
         [(v_factor.shape, BF16)],
         16,
-    )(rhs, v_factor, mix_first, turn)
+    )(rhs, v_factor, mix_first)
 
     def first_mix(z):
-        return call(first_mix_kernel, [VMEM, VMEM, SMEM], [t1_out])(z, mix_kept, turn)
+        return call(first_mix_kernel, [VMEM, VMEM], [t1_out])(z, mix_kept)
 
     z = exchange(z, COL)
     t1 = exchange(first_mix(z), ROW)
     t1, place = lax.optimization_barrier((t1, place))
-    near_wide, uc, near_first = call(
-        first_near_kernel,
-        [VMEM, VMEM, VMEM, VMEM, VMEM, SMEM, SMEM],
-        [(KEPT, *wide_shape, VMEM), (KEPT, *uc_shape, VMEM), (KEPT, *field, VMEM)],
-        [store, store],
-    )(near_rows, u_factor, rhs_kept, z, t1, turn, place)
-    d, z = call(
-        second_mix_kernel, [VMEM] * 5 + [SMEM], [(KEPT, *field, VMEM), z_out], [t2_shape]
-    )(t1, mix_second, uc, near_first, vc, turn)
+    near_wide, uc, d, z = call(
+        first_apply_kernel,
+        [VMEM, VMEM, VMEM, VMEM, VMEM, HBM, VMEM, VMEM],
+        [(KEPT, *wide_shape, VMEM), (KEPT, *uc_shape, VMEM), (KEPT, *field, VMEM), z_out],
+        [field, store, store, t2_shape],
+        table=place,
+    )(near_rows, u_factor, rhs_kept, z, t1, place, mix_second, vc)
     z = exchange(z, COL)
     t1 = exchange(first_mix(z), ROW)
-    near_second = call(
-        near_kernel, [VMEM, VMEM, VMEM, SMEM, SMEM, VMEM], [(KEPT, *field, VMEM)], [store, store]
-    )(d, z, t1, turn, place, near_wide)
     e, sums = call(
-        last_mix_kernel,
-        [VMEM] * 6,
+        second_apply_kernel,
+        [VMEM, VMEM, VMEM, VMEM, VMEM, HBM, VMEM, VMEM],
         [(KEPT, *field, VMEM), (KEPT, (devices, 1, 8 * RHS), F32, VMEM)],
-        [t2_shape],
-    )(t1, mix_second, uc, near_second, rhs_kept, d)
+        [field, store, store, t2_shape],
+        table=place,
+    )(t1, mix_second, uc, near_wide, z, place, rhs_kept, d)
     sums = exchange(sums, ROW_COL)
     return tuple(
         call(

time: 93.1 us -> 89.6 us (0.962)
  Pallas kernels: 18.6 us -> 15.4 us
    pallas_call x8 -> x6, Pallas kernels: 18.6 us -> 15.4 us  [placed(): out = run(*args)]
where the time goes in v3:
time: 89.6 us; the launch traced here: 89.3 us
  blocking collectives  73.2 us (82%)
  Pallas kernels  15.4 us (17%)
    all_to_all x5, blocking collectives, exchange(): return lax.all_to_all(x, axes, split_axis=0, concat_axis=0, tiled=True)  73.2 us
    pallas_call x6, Pallas kernels, placed(): out = run(*args)  15.4 us

profile of v3, /device:TPU:1, one launch (start us, length us, event | category | flops | bytes accessed | tf_op | source)
XLA Modules:
  0.0 89.3 jit_solution(3675267619436401379)
XLA Ops:
  0.6 3.7 %spread_v_kernel.1 = (bf16[32,64,128]{2,1,0:T(8,128)(2,1)S(1)}, bf16[16,32,512]{2,1,0:T(8,128)(2,1)S(1)}, f32[32,8192]{1,0:T(8,128)S(1)}, bf16[8,512,512]{2,1,0:T(8,128)(2,1)S(1)}) custom-call(f32[32,8192]{1,0:T(8,128)} %rhs_hbm.1, bf16[128,2048]{1,0:T(8,128)(2,1)} %v_hbm.1, bf16[8,512,512]{2,1,0:T(8,128)(2,1)} %bitcast.11), custom_call_target="tpu_custom_call" | custom-call | flops 1000000 | bytes 1000000 | tf_op jit(solution)/shard_map/spread_v_kernel/pallas_call | solution.py:398
  4.3 0.0 copy-start
  4.3 0.0 copy-start.1
  4.3 0.0 copy-start.2
  4.4 19.1 %all_to_all.25.z_ref.in_ref = bf16[16,32,512]{2,1,0:T(8,128)(2,1)S(1)} all-to-all(bf16[16,32,512]{2,1,0:T(8,128)(2,1)S(1)} %get-tuple-element.15), channel_id=1, replica_groups=mesh['row_0'=4,'row_1'=2,'col_0'=4,'col_1'=4] {'col_0','col_1'}, dimensions={0} | all-to-all | bytes 1048576 | tf_op jit(solution)/shard_map/all_to_all | solution.py:429
  23.4 0.9 %first_mix_kernel.2 = bf16[8,32,768]{2,1,0:T(8,128)(2,1)S(1)} custom-call(bf16[16,32,512]{2,1,0:T(8,128)(2,1)S(1)} %all_to_all.25.z_ref.in_ref, bf16[8,512,512]{2,1,0:T(8,128)(2,1)S(1)} %get-tuple-element.16.mix_ref), custom_call_target="tpu_custom_call" | custom-call | flops 1000000 | bytes 1000000 | tf_op jit(solution)/shard_map/first_mix_kernel/pallas_call | solution.py:398
  24.4 14.2 %all_to_all.26.t1_ref = bf16[8,32,768]{2,1,0:T(8,128)(2,1)S(1)} all-to-all(bf16[8,32,768]{2,1,0:T(8,128)(2,1)S(1)} %first_mix_kernel.2), channel_id=1, replica_groups=mesh['row_0'=4,'row_1'=2,'col_0'=4,'col_1'=4] {'row_0','row_1'}, dimensions={0} | all-to-all | bytes 786432 | tf_op jit(solution)/shard_map/all_to_all | solution.py:429
  38.6 0.0 copy-done
  38.6 0.0 copy-done.1
  38.6 0.0 copy-done.2
  38.6 5.2 %first_apply_kernel.1 = (bf16[64,128,256]{2,1,0:T(8,128)(2,1)S(1)}, bf16[32,32,256]{2,1,0:T(8,128)(2,1)S(1)}, f32[32,8192]{1,0:T(8,128)S(1)}, bf16[16,32,512]{2,1,0:T(8,128)(2,1)S(1)}) custom-call(bf16[128,128,128]{2,1,0:T(8,128)(2,1)S(1)} %bitcast.10, bf16[128,2048]{1,0:T(8,128)(2,1)S(1)} %copy-done.2, f32[32,8192]{1,0:T(8,128)S(1)} %get-tuple-element.14.v_ref.rhs_ref, ...), custom_call_target="tpu_custom_call" | custom-call | flops 1000000 | bytes 1000000 | tf_op jit(solution)/shard_map/first_apply_kernel/pallas_call | solution.py:398
  43.8 13.2 %all_to_all.27.z_ref.in_ref = bf16[16,32,512]{2,1,0:T(8,128)(2,1)S(1)} all-to-all(bf16[16,32,512]{2,1,0:T(8,128)(2,1)S(1)} %get-tuple-element.20), channel_id=1, replica_groups=mesh['row_0'=4,'row_1'=2,'col_0'=4,'col_1'=4] {'col_0','col_1'}, dimensions={0} | all-to-all | bytes 1048576 | tf_op jit(solution)/shard_map/all_to_all | solution.py:429
  57.0 0.9 %first_mix_kernel.3 = bf16[8,32,768]{2,1,0:T(8,128)(2,1)S(1)} custom-call(bf16[16,32,512]{2,1,0:T(8,128)(2,1)S(1)} %all_to_all.27.z_ref.in_ref, bf16[8,512,512]{2,1,0:T(8,128)(2,1)S(1)} %get-tuple-element.16.mix_ref), custom_call_target="tpu_custom_call" | custom-call | flops 1000000 | bytes 1000000 | tf_op jit(solution)/shard_map/first_mix_kernel/pallas_call | solution.py:398
  57.9 12.4 %all_to_all.28.t1_ref = bf16[8,32,768]{2,1,0:T(8,128)(2,1)S(1)} all-to-all(bf16[8,32,768]{2,1,0:T(8,128)(2,1)S(1)} %first_mix_kernel.3), channel_id=1, replica_groups=mesh['row_0'=4,'row_1'=2,'col_0'=4,'col_1'=4] {'row_0','row_1'}, dimensions={0} | all-to-all | bytes 786432 | tf_op jit(solution)/shard_map/all_to_all | solution.py:429
  70.3 3.0 %second_apply_kernel.1 = (f32[32,8192]{1,0:T(8,128)S(1)}, f32[128,1,256]{2,1,0:T(1,128)S(1)}) custom-call(bf16[8,32,768]{2,1,0:T(8,128)(2,1)S(1)} %all_to_all.28.t1_ref, bf16[16,256,256]{2,1,0:T(8,128)(2,1)S(1)} %bitcast.9, bf16[32,32,256]{2,1,0:T(8,128)(2,1)S(1)} %get-tuple-element.21.uc_ref, bf16[64,128,256]{2,1,0:T(8,128)(2,1)S(1)} %get-tuple-element.22.wide_ref, ...), custom_call_target="tpu_custom_call" | custom-call | flops 1000000 | bytes 1000000 | tf_op jit(solution)/shard_map/second_apply_kernel/pallas_call | solution.py:398
  73.3 14.3 %all_to_all.29.sums_ref = f32[128,1,256]{2,1,0:T(1,128)S(1)} all-to-all(f32[128,1,256]{2,1,0:T(1,128)S(1)} %get-tuple-element.24), channel_id=1, replica_groups=mesh['row_0'=4,'row_1'=2,'col_0'=4,'col_1'=4] {'row_0','row_1','col_0','..., dimensions={0} | all-to-all | bytes 262144 | tf_op jit(solution)/shard_map/all_to_all | solution.py:429
  87.6 1.7 %finish_kernel.1 = (f32[32,8192]{1,0:T(8,128)}, f32[32,8192]{1,0:T(8,128)}) custom-call(f32[128,1,256]{2,1,0:T(1,128)S(1)} %all_to_all.29.sums_ref, f32[32,8192]{1,0:T(8,128)S(1)} %get-tuple-element.14.v_ref.rhs_ref, f32[32,8192]{1,0:T(8,128)S(1)} %get-tuple-element.23.d_ref, f32[32,8192]{1,0:T(8,128)S(1)} %get-tuple-element.25.e_ref), custom_call_target="tpu_custom_call" | custom-call | flops 1000000 | bytes 1000000 | tf_op jit(solution)/shard_map/finish_kernel/pallas_call | solution.py:398
Async XLA Ops:
  4.3 34.2 %copy-start = (bf16[1,16,256,256]{3,2,1,0:T(8,128)(2,1)S(1)}, bf16[1,16,256,256]{3,2,1,0:T(8,128)(2,1)}, u32[]{:S(2)}) copy-start(bf16[1,16,256,256]{3,2,1,0:T(8,128)(2,1)} %param.12) | copy-start | bytes 6291460
  4.3 34.2 %copy-start.1 = (bf16[128,4,4096]{2,1,0:T(4,128)(2,1)S(1)}, bf16[128,4,4096]{2,1,0:T(4,128)(2,1)}, u32[]{:S(2)}) copy-start(bf16[128,4,4096]{2,1,0:T(4,128)(2,1)} %param.8) | copy-start | bytes 12582916
  4.3 34.2 %copy-start.2 = (bf16[128,2048]{1,0:T(8,128)(2,1)S(1)}, bf16[128,2048]{1,0:T(8,128)(2,1)}, u32[]{:S(2)}) copy-start(bf16[128,2048]{1,0:T(8,128)(2,1)} %u_ref.1) | copy-start | bytes 1572868

commit v4 on v3

--- a/solution.py
+++ b/solution.py
@@ -167,7 +167,7 @@
                 out_ref[pair, leaf * LEAF + 32 : leaf * LEAF + 64, lanes] = odd.astype(BF16)
 
 
-def near_product(v_ref, z_ref, t1_ref, place_ref, near_ref, out_ref, left, right, table):
+def near_product(v_ref, z_ref, t1_ref, place_ref, near_ref, out_ref, held, table):
     half = lane_half(RHS)
     lane = lax.broadcasted_iota(jnp.int32, (RHS, LANES), 1)
     order = lane // LEAF * LEAF + lane % 2 * 32 + lane % LEAF // 2
@@ -175,11 +175,8 @@
     tiles = v_ref.shape[1] // LANES
 
     def put(t, x):
-        turned = pltpu.roll(x, LEAF, 1)
-        left[2 * t] = jnp.where(half, x, 0.0).astype(BF16)
-        left[2 * t + 1] = jnp.where(half, turned, 0.0).astype(BF16)
-        right[2 * t] = jnp.where(half, 0.0, turned).astype(BF16)
-        right[2 * t + 1] = jnp.where(half, 0.0, x).astype(BF16)
+        held[2 * t] = x.astype(BF16)
+        held[2 * t + 1] = pltpu.roll(x, LEAF, 1).astype(BF16)
 
     column, row = column_index(), row_index()
     n_col, n_row = z_ref.shape[0], t1_ref.shape[0]
@@ -202,7 +199,15 @@
     for pair in range(tiles):
         lhs = [
             jnp.concatenate(
-                [left[place_ref[2 * h, leaf] + (leaf + HALO)] + right[place_ref[2 * h + 1, leaf] + (leaf + HALO)] for h in range(2)], axis=1
+                [
+                    jnp.where(
+                        half,
+                        held[place_ref[2 * h, leaf] + (leaf + HALO)],
+                        held[(place_ref[2 * h + 1, leaf] + (leaf + HALO)) ^ 1],
+                    )
+                    for h in range(2)
+                ],
+                axis=1,
             )
             for leaf in (2 * pair, 2 * pair + 1)
         ]
@@ -287,14 +292,14 @@
 def first_apply_kernel(
     rows_ref, u_ref, v_ref, in_ref, t1_ref, place_hbm, mix_ref, vc_ref,
     wide_ref, uc_ref, d_ref, z_ref,
-    near_ref, left, right, t2_ref, place_ref, sem,
+    near_ref, held, t2_ref, place_ref, sem,
 ):
     table = pltpu.make_async_copy(place_hbm, place_ref, sem)
     table.start()
     spread_near(rows_ref, wide_ref)
     spread_u(u_ref, uc_ref)
     second_mix(t1_ref, mix_ref, t2_ref)
-    near_product(v_ref, in_ref, t1_ref, place_ref, wide_ref, near_ref, left, right, table)
+    near_product(v_ref, in_ref, t1_ref, place_ref, wide_ref, near_ref, held, table)
     shift = column_index() % 4 * RANK
     groups = uc_ref.shape[0]
     masks = expand_masks()
@@ -312,12 +317,12 @@
 def second_apply_kernel(
     t1_ref, mix_ref, uc_ref, wide_ref, in_ref, place_hbm, rhs_ref, d_ref,
     e_ref, sums_ref,
-    near_ref, left, right, t2_ref, place_ref, sem,
+    near_ref, held, t2_ref, place_ref, sem,
 ):
     table = pltpu.make_async_copy(place_hbm, place_ref, sem)
     table.start()
     second_mix(t1_ref, mix_ref, t2_ref)
-    near_product(d_ref, in_ref, t1_ref, place_ref, wide_ref, near_ref, left, right, table)
+    near_product(d_ref, in_ref, t1_ref, place_ref, wide_ref, near_ref, held, table)
     masks = expand_masks()
     total = [jnp.zeros((RHS, LANES), F32) for _ in range(6)]
     for g in range(uc_ref.shape[0]):
@@ -448,7 +453,7 @@
         first_apply_kernel,
         [VMEM, VMEM, VMEM, VMEM, VMEM, HBM, VMEM, VMEM],
         [(KEPT, *wide_shape, VMEM), (KEPT, *uc_shape, VMEM), (KEPT, *field, VMEM), z_out],
-        [field, store, store, t2_shape],
+        [field, store, t2_shape],
         table=place,
     )(near_rows, u_factor, rhs_kept, z, t1, place, mix_second, vc)
     z = exchange(z, COL)
@@ -457,7 +462,7 @@
         second_apply_kernel,
         [VMEM, VMEM, VMEM, VMEM, VMEM, HBM, VMEM, VMEM],
         [(KEPT, *field, VMEM), (KEPT, (devices, 1, 8 * RHS), F32, VMEM)],
-        [field, store, store, t2_shape],
+        [field, store, t2_shape],
         table=place,
     )(t1, mix_second, uc, near_wide, z, place, rhs_kept, d)
     sums = exchange(sums, ROW_COL)

time: 89.6 us -> 89.4 us (level)
  no operation moved by 1% of the time
where the time goes in v4:
time: 89.4 us; the launch traced here: 89.1 us
  blocking collectives  73.2 us (82%)
  Pallas kernels  15.2 us (17%)
    all_to_all x5, blocking collectives, exchange(): return lax.all_to_all(x, axes, split_axis=0, concat_axis=0, tiled=True)  73.2 us
    pallas_call x6, Pallas kernels, placed(): out = run(*args)  15.2 us

profile of v4, /device:TPU:1, one launch (start us, length us, event | category | flops | bytes accessed | tf_op | source)
XLA Modules:
  0.0 89.1 jit_solution(15304255727293334101)
XLA Ops:
  0.6 3.7 %spread_v_kernel.1 = (bf16[32,64,128]{2,1,0:T(8,128)(2,1)S(1)}, bf16[16,32,512]{2,1,0:T(8,128)(2,1)S(1)}, f32[32,8192]{1,0:T(8,128)S(1)}, bf16[8,512,512]{2,1,0:T(8,128)(2,1)S(1)}) custom-call(f32[32,8192]{1,0:T(8,128)} %rhs_hbm.1, bf16[128,2048]{1,0:T(8,128)(2,1)} %v_hbm.1, bf16[8,512,512]{2,1,0:T(8,128)(2,1)} %bitcast.11), custom_call_target="tpu_custom_call" | custom-call | flops 1000000 | bytes 1000000 | tf_op jit(solution)/shard_map/spread_v_kernel/pallas_call | solution.py:403
  4.3 0.0 copy-start
  4.3 0.0 copy-start.1
  4.3 0.0 copy-start.2
  4.4 19.1 %all_to_all.25.z_ref.in_ref = bf16[16,32,512]{2,1,0:T(8,128)(2,1)S(1)} all-to-all(bf16[16,32,512]{2,1,0:T(8,128)(2,1)S(1)} %get-tuple-element.15), channel_id=1, replica_groups=mesh['row_0'=4,'row_1'=2,'col_0'=4,'col_1'=4] {'col_0','col_1'}, dimensions={0} | all-to-all | bytes 1048576 | tf_op jit(solution)/shard_map/all_to_all | solution.py:434
  23.4 0.9 %first_mix_kernel.2 = bf16[8,32,768]{2,1,0:T(8,128)(2,1)S(1)} custom-call(bf16[16,32,512]{2,1,0:T(8,128)(2,1)S(1)} %all_to_all.25.z_ref.in_ref, bf16[8,512,512]{2,1,0:T(8,128)(2,1)S(1)} %get-tuple-element.16.mix_ref), custom_call_target="tpu_custom_call" | custom-call | flops 1000000 | bytes 1000000 | tf_op jit(solution)/shard_map/first_mix_kernel/pallas_call | solution.py:403
  24.4 14.2 %all_to_all.26.t1_ref = bf16[8,32,768]{2,1,0:T(8,128)(2,1)S(1)} all-to-all(bf16[8,32,768]{2,1,0:T(8,128)(2,1)S(1)} %first_mix_kernel.2), channel_id=1, replica_groups=mesh['row_0'=4,'row_1'=2,'col_0'=4,'col_1'=4] {'row_0','row_1'}, dimensions={0} | all-to-all | bytes 786432 | tf_op jit(solution)/shard_map/all_to_all | solution.py:434
  38.6 0.0 copy-done
  38.6 0.0 copy-done.1
  38.6 0.0 copy-done.2
  38.6 5.0 %first_apply_kernel.1 = (bf16[64,128,256]{2,1,0:T(8,128)(2,1)S(1)}, bf16[32,32,256]{2,1,0:T(8,128)(2,1)S(1)}, f32[32,8192]{1,0:T(8,128)S(1)}, bf16[16,32,512]{2,1,0:T(8,128)(2,1)S(1)}) custom-call(bf16[128,128,128]{2,1,0:T(8,128)(2,1)S(1)} %bitcast.10, bf16[128,2048]{1,0:T(8,128)(2,1)S(1)} %copy-done.2, f32[32,8192]{1,0:T(8,128)S(1)} %get-tuple-element.14.v_ref.rhs_ref, ...), custom_call_target="tpu_custom_call" | custom-call | flops 1000000 | bytes 1000000 | tf_op jit(solution)/shard_map/first_apply_kernel/pallas_call | solution.py:403
  43.6 13.2 %all_to_all.27.z_ref.in_ref = bf16[16,32,512]{2,1,0:T(8,128)(2,1)S(1)} all-to-all(bf16[16,32,512]{2,1,0:T(8,128)(2,1)S(1)} %get-tuple-element.20), channel_id=1, replica_groups=mesh['row_0'=4,'row_1'=2,'col_0'=4,'col_1'=4] {'col_0','col_1'}, dimensions={0} | all-to-all | bytes 1048576 | tf_op jit(solution)/shard_map/all_to_all | solution.py:434
  56.8 0.9 %first_mix_kernel.3 = bf16[8,32,768]{2,1,0:T(8,128)(2,1)S(1)} custom-call(bf16[16,32,512]{2,1,0:T(8,128)(2,1)S(1)} %all_to_all.27.z_ref.in_ref, bf16[8,512,512]{2,1,0:T(8,128)(2,1)S(1)} %get-tuple-element.16.mix_ref), custom_call_target="tpu_custom_call" | custom-call | flops 1000000 | bytes 1000000 | tf_op jit(solution)/shard_map/first_mix_kernel/pallas_call | solution.py:403
  57.7 12.4 %all_to_all.28.t1_ref = bf16[8,32,768]{2,1,0:T(8,128)(2,1)S(1)} all-to-all(bf16[8,32,768]{2,1,0:T(8,128)(2,1)S(1)} %first_mix_kernel.3), channel_id=1, replica_groups=mesh['row_0'=4,'row_1'=2,'col_0'=4,'col_1'=4] {'row_0','row_1'}, dimensions={0} | all-to-all | bytes 786432 | tf_op jit(solution)/shard_map/all_to_all | solution.py:434
  70.1 3.0 %second_apply_kernel.1 = (f32[32,8192]{1,0:T(8,128)S(1)}, f32[128,1,256]{2,1,0:T(1,128)S(1)}) custom-call(bf16[8,32,768]{2,1,0:T(8,128)(2,1)S(1)} %all_to_all.28.t1_ref, bf16[16,256,256]{2,1,0:T(8,128)(2,1)S(1)} %bitcast.9, bf16[32,32,256]{2,1,0:T(8,128)(2,1)S(1)} %get-tuple-element.21.uc_ref, bf16[64,128,256]{2,1,0:T(8,128)(2,1)S(1)} %get-tuple-element.22.wide_ref, ...), custom_call_target="tpu_custom_call" | custom-call | flops 1000000 | bytes 1000000 | tf_op jit(solution)/shard_map/second_apply_kernel/pallas_call | solution.py:403
  73.1 14.3 %all_to_all.29.sums_ref = f32[128,1,256]{2,1,0:T(1,128)S(1)} all-to-all(f32[128,1,256]{2,1,0:T(1,128)S(1)} %get-tuple-element.24), channel_id=1, replica_groups=mesh['row_0'=4,'row_1'=2,'col_0'=4,'col_1'=4] {'row_0','row_1','col_0','..., dimensions={0} | all-to-all | bytes 262144 | tf_op jit(solution)/shard_map/all_to_all | solution.py:434
  87.4 1.7 %finish_kernel.1 = (f32[32,8192]{1,0:T(8,128)}, f32[32,8192]{1,0:T(8,128)}) custom-call(f32[128,1,256]{2,1,0:T(1,128)S(1)} %all_to_all.29.sums_ref, f32[32,8192]{1,0:T(8,128)S(1)} %get-tuple-element.14.v_ref.rhs_ref, f32[32,8192]{1,0:T(8,128)S(1)} %get-tuple-element.23.d_ref, f32[32,8192]{1,0:T(8,128)S(1)} %get-tuple-element.25.e_ref), custom_call_target="tpu_custom_call" | custom-call | flops 1000000 | bytes 1000000 | tf_op jit(solution)/shard_map/finish_kernel/pallas_call | solution.py:403
Async XLA Ops:
  4.3 34.2 %copy-start = (bf16[1,16,256,256]{3,2,1,0:T(8,128)(2,1)S(1)}, bf16[1,16,256,256]{3,2,1,0:T(8,128)(2,1)}, u32[]{:S(2)}) copy-start(bf16[1,16,256,256]{3,2,1,0:T(8,128)(2,1)} %param.12) | copy-start | bytes 6291460
  4.3 34.2 %copy-start.1 = (bf16[128,4,4096]{2,1,0:T(4,128)(2,1)S(1)}, bf16[128,4,4096]{2,1,0:T(4,128)(2,1)}, u32[]{:S(2)}) copy-start(bf16[128,4,4096]{2,1,0:T(4,128)(2,1)} %param.8) | copy-start | bytes 12582916
  4.3 34.2 %copy-start.2 = (bf16[128,2048]{1,0:T(8,128)(2,1)S(1)}, bf16[128,2048]{1,0:T(8,128)(2,1)}, u32[]{:S(2)}) copy-start(bf16[128,2048]{1,0:T(8,128)(2,1)} %u_ref.1) | copy-start | bytes 1572868

commit v5 on v4

--- a/solution.py
+++ b/solution.py
@@ -105,36 +105,35 @@
     z_ref[lax.rem(column_index() + n_col - 1, n_col), :, width - edge :] = v_ref[:, :edge].astype(BF16)
 
 
-def spread_v_kernel(rhs_hbm, v_hbm, mix_hbm, vc_ref, z_ref, rhs_ref, mix_ref, v_ref, sems):
+def spread_v_kernel(rhs_hbm, v_hbm, vc_ref, z_ref, rhs_ref, v_ref, sems):
     queue = Queue(pieces_of(v_hbm, v_ref, sems, 0, 4) + pieces_of(rhs_hbm, rhs_ref, sems, 4, 4, 1), 8)
-    mix_in = pieces_of(mix_hbm, mix_ref, sems, 8, 8)
-    for copy in mix_in:
-        copy.start()
     group = lane_group(16)
     shift = column_index() % 4 * RANK
     order = row_order(256, 16)
     groups = vc_ref.shape[0]
+    masks = group_masks(LEAF)
+    lanes = v_order()
+    queue.wait(8)
     for sixteen in range(groups // 4):
-        if sixteen % (groups // 16) == 0:
-            queue.wait()
         rows = leaf_rows(v_ref, sixteen, order)
         for h in range(4):
+            g = 4 * sixteen + h
             of_leaf = [rows[16 * leaf : 16 * (leaf + 1)] for leaf in range(4 * h, 4 * h + 4)]
+            narrow = []
             for ur in range(4):
                 x = of_leaf[ur]
                 for leaf in range(4):
                     if leaf != ur:
                         x = jnp.where(group == leaf, pltpu.roll(of_leaf[leaf], (leaf - ur) * RANK % LANES, 1), x)
-                vc_ref[4 * sixteen + h, 16 * ur : 16 * (ur + 1), :] = x.astype(BF16)
-    masks = group_masks(LEAF)
-    lanes = v_order()
-    for g in range(groups):
-        if g % (groups // 4) == 0:
-            queue.wait()
-        part = compress(rhs_ref[:, 256 * g : 256 * (g + 1)], vc_ref[g], lanes, masks)
-        z_ref[g // 2, :, (g % 2) * LANES : (g % 2 + 1) * LANES] = pltpu.roll(part, shift, 1).astype(BF16)
+                narrow.append(x.astype(BF16))
+            narrow = jnp.concatenate(narrow, axis=0)
+            vc_ref[g] = narrow
+            part = compress(rhs_ref[:, 256 * g : 256 * (g + 1)], narrow, lanes, masks)
+            z_ref[g // 2, :, (g % 2) * LANES : (g % 2 + 1) * LANES] = pltpu.roll(part, shift, 1).astype(BF16)
+
+
+def edges_kernel(rhs_ref, z_in_ref, z_ref):
     put_edges(rhs_ref, z_ref)
-    wait_all(mix_in)
 
 
 def spread_u(u_ref, uc_ref):
@@ -380,7 +379,7 @@
 FAR_OFF = pltpu.HBM
 
 
-def call(kernel, in_specs, outs, scratch=(), sems=0, limit=8, table=None):
+def call(kernel, in_specs, outs, scratch=(), sems=0, limit=8, table=None, flops=1_000_000, aliases=None):
     run = pl.pallas_call(
         kernel,
         in_specs=in_specs,
@@ -389,7 +388,8 @@
         scratch_shapes=[pltpu.VMEM(*x) for x in scratch]
         + [pltpu.SemaphoreType.DMA((sems,))] * (sems > 0)
         + ([] if table is None else [pltpu.SMEM(table.shape, table.dtype), pltpu.SemaphoreType.DMA]),
-        cost_estimate=pl.CostEstimate(flops=1_000_000, bytes_accessed=1_000_000, transcendentals=0),
+        cost_estimate=pl.CostEstimate(flops=flops, bytes_accessed=max(1_000_000, flops // 1000), transcendentals=0),
+        input_output_aliases=aliases or {},
         compiler_params=pltpu.CompilerParams(vmem_limit_bytes=limit * MIB),
         name=kernel.__name__,
     )
@@ -435,16 +435,17 @@
 
     store = ((leaves + 2 * HALO, RHS, LANES), BF16)
 
-    vc, z, rhs_kept, mix_kept = call(
+    vc, z, rhs_kept = call(
         spread_v_kernel,
-        [HBM, HBM, HBM],
-        [(KEPT, *vc_shape, VMEM), z_out, (KEPT, *field, VMEM), (KEPT, mix_first.shape, BF16, VMEM)],
+        [HBM, HBM],
+        [(KEPT, *vc_shape, VMEM), z_out, (KEPT, *field, VMEM)],
         [(v_factor.shape, BF16)],
-        16,
-    )(rhs, v_factor, mix_first)
+        8,
+    )(rhs, v_factor)
+    z = call(edges_kernel, [VMEM, VMEM], [z_out], flops=20_000_000_000, aliases={1: 0})(rhs_kept, z)
 
     def first_mix(z):
-        return call(first_mix_kernel, [VMEM, VMEM], [t1_out])(z, mix_kept)
+        return call(first_mix_kernel, [VMEM, VMEM], [t1_out])(z, mix_first)
 
     z = exchange(z, COL)
     t1 = exchange(first_mix(z), ROW)

time: 89.4 us -> 88.3 us (0.988)
  Pallas kernels: 15.2 us -> 14.1 us
    pallas_call x6 -> x7, Pallas kernels: 15.2 us -> 14.1 us  [placed(): out = run(*args)]
where the time goes in v5:
time: 88.3 us; the launch traced here: 88 us
  blocking collectives  73.2 us (83%)
  Pallas kernels  14.1 us (16%)
    all_to_all x5, blocking collectives, exchange(): return lax.all_to_all(x, axes, split_axis=0, concat_axis=0, tiled=True)  73.2 us
    pallas_call x7, Pallas kernels, placed(): out = run(*args)  14.1 us

profile of v5, /device:TPU:1, one launch (start us, length us, event | category | flops | bytes accessed | tf_op | source)
XLA Modules:
  0.0 88.0 jit_solution(5229945620860523339)
XLA Ops:
  0.6 2.5 %spread_v_kernel.1 = (bf16[32,64,128]{2,1,0:T(8,128)(2,1)S(1)}, bf16[16,32,512]{2,1,0:T(8,128)(2,1)S(1)}, f32[32,8192]{1,0:T(8,128)S(1)}) custom-call(f32[32,8192]{1,0:T(8,128)} %rhs_hbm.1, bf16[128,2048]{1,0:T(8,128)(2,1)} %v_hbm.1), custom_call_target="tpu_custom_call" | custom-call | flops 1000000 | bytes 1000000 | tf_op jit(solution)/shard_map/spread_v_kernel/pallas_call | solution.py:403
  3.1 0.0 copy-start
  3.2 0.0 copy-start.1
  3.2 0.0 copy-start.2
  3.2 0.0 copy-start.3
  3.2 19.1 %all_to_all.25.z_ref.in_ref = bf16[16,32,512]{2,1,0:T(8,128)(2,1)S(1)} all-to-all(bf16[16,32,512]{2,1,0:T(8,128)(2,1)S(1)} %edges_kernel.1), channel_id=1, replica_groups=mesh['row_0'=4,'row_1'=2,'col_0'=4,'col_1'=4] {'col_0','col_1'}, dimensions={0} | all-to-all | bytes 1048576 | tf_op jit(solution)/shard_map/all_to_all | solution.py:434
  22.3 0.0 copy-done
  22.3 0.9 %first_mix_kernel.2 = bf16[8,32,768]{2,1,0:T(8,128)(2,1)S(1)} custom-call(bf16[16,32,512]{2,1,0:T(8,128)(2,1)S(1)} %all_to_all.25.z_ref.in_ref, bf16[8,512,512]{2,1,0:T(8,128)(2,1)S(1)} %bitcast.8), custom_call_target="tpu_custom_call" | custom-call | flops 1000000 | bytes 1000000 | tf_op jit(solution)/shard_map/first_mix_kernel/pallas_call | solution.py:403
  23.2 14.2 %all_to_all.26.t1_ref = bf16[8,32,768]{2,1,0:T(8,128)(2,1)S(1)} all-to-all(bf16[8,32,768]{2,1,0:T(8,128)(2,1)S(1)} %first_mix_kernel.2), channel_id=1, replica_groups=mesh['row_0'=4,'row_1'=2,'col_0'=4,'col_1'=4] {'row_0','row_1'}, dimensions={0} | all-to-all | bytes 786432 | tf_op jit(solution)/shard_map/all_to_all | solution.py:434
  37.4 0.0 copy-done.1
  37.4 0.0 copy-done.2
  37.4 0.0 copy-done.3
  37.4 5.0 %first_apply_kernel.1 = (bf16[64,128,256]{2,1,0:T(8,128)(2,1)S(1)}, bf16[32,32,256]{2,1,0:T(8,128)(2,1)S(1)}, f32[32,8192]{1,0:T(8,128)S(1)}, bf16[16,32,512]{2,1,0:T(8,128)(2,1)S(1)}) custom-call(bf16[128,128,128]{2,1,0:T(8,128)(2,1)S(1)} %bitcast.12, bf16[128,2048]{1,0:T(8,128)(2,1)S(1)} %copy-done.3, f32[32,8192]{1,0:T(8,128)S(1)} %get-tuple-element.13.rhs_ref.v_ref, ...), custom_call_target="tpu_custom_call" | custom-call | flops 1000000 | bytes 1000000 | tf_op jit(solution)/shard_map/first_apply_kernel/pallas_call | solution.py:403
  42.4 13.2 %all_to_all.27.z_ref.in_ref = bf16[16,32,512]{2,1,0:T(8,128)(2,1)S(1)} all-to-all(bf16[16,32,512]{2,1,0:T(8,128)(2,1)S(1)} %get-tuple-element.18), channel_id=1, replica_groups=mesh['row_0'=4,'row_1'=2,'col_0'=4,'col_1'=4] {'col_0','col_1'}, dimensions={0} | all-to-all | bytes 1048576 | tf_op jit(solution)/shard_map/all_to_all | solution.py:434
  55.6 0.9 %first_mix_kernel.3 = bf16[8,32,768]{2,1,0:T(8,128)(2,1)S(1)} custom-call(bf16[16,32,512]{2,1,0:T(8,128)(2,1)S(1)} %all_to_all.27.z_ref.in_ref, bf16[8,512,512]{2,1,0:T(8,128)(2,1)S(1)} %bitcast.9), custom_call_target="tpu_custom_call" | custom-call | flops 1000000 | bytes 1000000 | tf_op jit(solution)/shard_map/first_mix_kernel/pallas_call | solution.py:403
  56.5 12.4 %all_to_all.28.t1_ref = bf16[8,32,768]{2,1,0:T(8,128)(2,1)S(1)} all-to-all(bf16[8,32,768]{2,1,0:T(8,128)(2,1)S(1)} %first_mix_kernel.3), channel_id=1, replica_groups=mesh['row_0'=4,'row_1'=2,'col_0'=4,'col_1'=4] {'row_0','row_1'}, dimensions={0} | all-to-all | bytes 786432 | tf_op jit(solution)/shard_map/all_to_all | solution.py:434
  68.9 3.1 %second_apply_kernel.1 = (f32[32,8192]{1,0:T(8,128)S(1)}, f32[128,1,256]{2,1,0:T(1,128)S(1)}) custom-call(bf16[8,32,768]{2,1,0:T(8,128)(2,1)S(1)} %all_to_all.28.t1_ref, bf16[16,256,256]{2,1,0:T(8,128)(2,1)S(1)} %bitcast.11, bf16[32,32,256]{2,1,0:T(8,128)(2,1)S(1)} %get-tuple-element.19.uc_ref, bf16[64,128,256]{2,1,0:T(8,128)(2,1)S(1)} %get-tuple-element.20.wide_ref, ...), custom_call_target="tpu_custom_call" | custom-call | flops 1000000 | bytes 1000000 | tf_op jit(solution)/shard_map/second_apply_kernel/pallas_call | solution.py:403
  72.0 14.3 %all_to_all.29.sums_ref = f32[128,1,256]{2,1,0:T(1,128)S(1)} all-to-all(f32[128,1,256]{2,1,0:T(1,128)S(1)} %get-tuple-element.22), channel_id=1, replica_groups=mesh['row_0'=4,'row_1'=2,'col_0'=4,'col_1'=4] {'row_0','row_1','col_0','..., dimensions={0} | all-to-all | bytes 262144 | tf_op jit(solution)/shard_map/all_to_all | solution.py:434
  86.3 1.7 %finish_kernel.1 = (f32[32,8192]{1,0:T(8,128)}, f32[32,8192]{1,0:T(8,128)}) custom-call(f32[128,1,256]{2,1,0:T(1,128)S(1)} %all_to_all.29.sums_ref, f32[32,8192]{1,0:T(8,128)S(1)} %get-tuple-element.13.rhs_ref.v_ref, f32[32,8192]{1,0:T(8,128)S(1)} %get-tuple-element.21.d_ref, f32[32,8192]{1,0:T(8,128)S(1)} %get-tuple-element.23.e_ref), custom_call_target="tpu_custom_call" | custom-call | flops 1000000 | bytes 1000000 | tf_op jit(solution)/shard_map/finish_kernel/pallas_call | solution.py:403
  (1 shorter events, 0.0 us)
Async XLA Ops:
  3.1 19.2 %copy-start = (bf16[1,8,512,512]{3,2,1,0:T(8,128)(2,1)S(1)}, bf16[1,8,512,512]{3,2,1,0:T(8,128)(2,1)}, u32[]{:S(2)}) copy-start(bf16[1,8,512,512]{3,2,1,0:T(8,128)(2,1)} %param.11) | copy-start | bytes 12582916
  3.2 34.2 %copy-start.1 = (bf16[1,16,256,256]{3,2,1,0:T(8,128)(2,1)S(1)}, bf16[1,16,256,256]{3,2,1,0:T(8,128)(2,1)}, u32[]{:S(2)}) copy-start(bf16[1,16,256,256]{3,2,1,0:T(8,128)(2,1)} %param.12) | copy-start | bytes 6291460
  3.2 34.2 %copy-start.2 = (bf16[128,4,4096]{2,1,0:T(4,128)(2,1)S(1)}, bf16[128,4,4096]{2,1,0:T(4,128)(2,1)}, u32[]{:S(2)}) copy-start(bf16[128,4,4096]{2,1,0:T(4,128)(2,1)} %param.8) | copy-start | bytes 12582916
  3.2 34.2 %copy-start.3 = (bf16[128,2048]{1,0:T(8,128)(2,1)S(1)}, bf16[128,2048]{1,0:T(8,128)(2,1)}, u32[]{:S(2)}) copy-start(bf16[128,2048]{1,0:T(8,128)(2,1)} %u_ref.1) | copy-start | bytes 1572868
